TPU v7x, 256 devices: a whole 4x4x8 slice. The times are simulated.
256 devices in a mesh: pix: 32 (over z_hi, x, core), rep: 8 (over y, z_lo).
Axes of the slice: x: 4, y: 4, z: 8 (z_hi: 4, z_lo: 2; z = z_hi * 2 + z_lo), core: 2. Of those that a mesh axis runs over, the one named last changes fastest.
Arguments:
- tokens: bfloat16 [2048, 16, 1152], P(('pix', 'rep')), may hold values from -48 to 48
- out_grad: bfloat16 [2048, 16, 1152], P(('pix', 'rep')), may hold values from -6 to 6
- query_weight: bfloat16 [1152, 1152], P('pix'), may hold values from -0.1875 to 0.1875
- key_weight: bfloat16 [1152, 1152], P('pix'), may hold values from -0.1875 to 0.1875
- value_weight: bfloat16 [1152, 1152], P('pix'), may hold values from -0.1875 to 0.1875
- output_weight: bfloat16 [1152, 1152], P('pix'), may hold values from -0.1875 to 0.1875
Outputs:
- input_grad: bfloat16 [2048, 16, 1152], P(('pix', 'rep'))
- weight_grads: float32 [1152, 4608], P('pix')
All inputs are finite; a program needn't handle non-finite values.
Results may differ from a plain program's by a relative error of at most 0.025.
The roundings to bfloat16 on the way count: a program that leaves them out, or rounds other values in their place, can miss the bound.
Values may be sent and summed in bfloat16 or wider, within the bound.
A program may use at most 128 MiB of HBM per device.

v0:
```python
import jax
import jax.numpy as jnp
from jax import lax
from jax.sharding import Mesh
from jax.sharding import PartitionSpec as P

D = 1152
HEADS = 16
HEAD_DIM = 72
FRAMES = 16
PIX = ("pix_0", "pix_1", "pix_2")
PIX_REP = ("pix_0", "pix_1", "pix_2", "rep")


def side_by_side(arrays, axis, dim, along):
    ends, at = ([], 0)
    for a in arrays[:-1]:
        at += a.shape[along]
        ends.append(at)
    both = jnp.concatenate(arrays, axis=along)
    return tuple(jnp.split(lax.all_gather(both, axis, axis=dim, tiled=True), ends, axis=along))


def in_blocks(value, dim, peers):
    before, after = (value.shape[:dim], value.shape[dim + 1 :])
    return jnp.moveaxis(value.reshape(*before, peers, -1, *after), dim, 0)


def sum_by_chip_2(value, chips, core, dim):
    sizes = (lax.axis_size(chips), lax.axis_size(core))
    pieces = in_blocks(value, dim, sizes[0] * sizes[1])
    inside = pieces.shape[1:]
    pieces = pieces.reshape(*sizes, *inside).swapaxes(0, 1).reshape(-1, *inside)
    pieces = lax.psum_scatter(pieces, core, scatter_dimension=0, tiled=True)
    return lax.psum_scatter(pieces, chips, scatter_dimension=0, tiled=True)[0]


def sent_to_all(value, axis):
    copies = jnp.broadcast_to(value, (lax.axis_size(axis), *value.shape))
    return lax.all_to_all(copies, axis, split_axis=0, concat_axis=0, tiled=True)


def taken_together(value, axis):
    return sent_to_all(value, axis).sum(axis=0)


def contract_last(left, right):
    return lax.dot_general(
        left, right, (((1,), (1,)), ((), ())), preferred_element_type=jnp.float32
    )


def contract_first(left, right):
    return lax.dot_general(
        left, right, (((0,), (0,)), ((), ())), preferred_element_type=jnp.float32
    )


def local(tokens, out_grad, query_weight, key_weight, value_weight, output_weight):
    count = tokens.shape[0]
    rows = tokens.reshape(-1, D)
    drows = out_grad.reshape(-1, D)
    scale = 1.0 / HEAD_DIM**0.5
    full_q, full_k, full_v, full_o = side_by_side(
        (query_weight, key_weight, value_weight, output_weight), PIX, 0, 1
    )
    query = jnp.dot(rows, full_q, preferred_element_type=jnp.float32).astype(jnp.bfloat16)
    keyed = jnp.dot(rows, full_k, preferred_element_type=jnp.float32).astype(jnp.bfloat16)
    valued = jnp.dot(rows, full_v, preferred_element_type=jnp.float32).astype(jnp.bfloat16)
    shape4 = (count, FRAMES, HEADS, HEAD_DIM)
    qh = query.reshape(shape4)
    kh = keyed.reshape(shape4)
    vh = valued.reshape(shape4)
    scores = jnp.einsum("sfhe,sghe->shfg", qh, kh, preferred_element_type=jnp.float32) * scale
    scores = scores - jnp.max(scores, axis=-1, keepdims=True)
    expo = jnp.exp(scores)
    probs = expo / jnp.sum(expo, axis=-1, keepdims=True)
    probs_b = probs.astype(jnp.bfloat16)
    attended = (
        jnp.einsum("shfg,sghe->sfhe", probs_b, vh, preferred_element_type=jnp.float32)
        .reshape(-1, D)
        .astype(jnp.bfloat16)
    )
    dattn = contract_last(drows, full_o).astype(jnp.bfloat16)
    dah = dattn.reshape(shape4)
    dvalue = (
        jnp.einsum("shfg,sfhe->sghe", probs_b, dah, preferred_element_type=jnp.float32)
        .reshape(-1, D)
        .astype(jnp.bfloat16)
    )
    dprobs = jnp.einsum("sfhe,sghe->shfg", dah, vh, preferred_element_type=jnp.float32)
    dscore = (probs * (dprobs - jnp.sum(dprobs * probs, axis=-1, keepdims=True)) * scale).astype(
        jnp.bfloat16
    )
    dquery = (
        jnp.einsum("shfg,sghe->sfhe", dscore, kh, preferred_element_type=jnp.float32)
        .reshape(-1, D)
        .astype(jnp.bfloat16)
    )
    dkey = (
        jnp.einsum("shfg,sfhe->sghe", dscore, qh, preferred_element_type=jnp.float32)
        .reshape(-1, D)
        .astype(jnp.bfloat16)
    )
    grads = sum_by_chip_2(
        jnp.concatenate(
            [
                jnp.concatenate(
                    [
                        contract_first(rows, dquery),
                        contract_first(rows, dkey),
                        contract_first(rows, dvalue),
                    ],
                    axis=1,
                ),
                contract_first(attended, drows),
            ],
            axis=1,
        ).astype(jnp.bfloat16),
        ("pix_0", "pix_1"),
        "pix_2",
        0,
    ).astype(jnp.float32)
    back_q, back_k, back_v = (full_q, full_k, full_v)
    dinput = (
        contract_last(dquery, back_q) + contract_last(dkey, back_k) + contract_last(dvalue, back_v)
    )
    weight_grads = taken_together(grads, "rep")
    return (dinput.astype(jnp.bfloat16).reshape(tokens.shape), weight_grads)


def solution(mesh):
    torus = Mesh(
        mesh.devices.reshape(4, 4, 2, mesh.shape["rep"]), ("pix_0", "pix_1", "pix_2", "rep")
    )
    placed = (
        P(PIX_REP, None, None),
        P(PIX_REP, None, None),
        P(PIX, None),
        P(PIX, None),
        P(PIX, None),
        P(PIX, None),
    )
    return jax.shard_map(
        local,
        mesh=torus,
        in_specs=placed,
        out_specs=(P(PIX_REP, None, None), P(PIX, None)),
        check_vma=False,
    )
```

profile of v0, /device:TPU:1, one launch (start us, length us, event | category | flops | bytes accessed | tf_op | source)
XLA Modules:
  0.0 420.6 jit_solution(10867099937794037141)
XLA Ops:
  9.1 92.7 %all-gather.3.cloned.1.call-done = bf16[32,36,4608]{2,1,0:T(8,128)(2,1)} async-done(((bf16[1,36,4608]{2,1,0:T(8,128)(2,1)}), bf16[32,36,4608]{2,1,0:T(8,128)(2,1)}) %all-gather.3.cloned.1.call-update) | async-done | bytes 10616848 | tf_op jit(solution)/shard_map/all_gather | solution.py:21
  101.8 13.9 %reshape.62 = bf16[1152,4608]{1,0:T(8,128)(2,1)} reshape(bf16[32,36,4608]{2,1,0:T(8,128)(2,1)} %all-gather.3.cloned.1.call-done) | data formatting | bytes 21233664
  115.8 2.7 fusion.13
  118.4 2.7 fusion.12
  121.1 2.7 fusion.11
  125.0 2.6 fusion.14
  146.9 2.6 fusion.4
  149.5 3.5 concatenate.17
  153.0 2.4 fusion.3
  155.4 5.1 %concatenate.16 = bf16[16,2,36,1152]{3,2,1,0:T(8,128)(2,1)} reshape(bf16[1152,1152]{1,0:T(8,128)(2,1)} %fusion.3) | data formatting | bytes 5308416 | tf_op jit(solution)/shard_map/concatenate | solution.py:106
  160.6 3.4 fusion.2
  164.0 5.1 %concatenate.15 = bf16[16,2,36,1152]{3,2,1,0:T(8,128)(2,1)} reshape(bf16[1152,1152]{1,0:T(8,128)(2,1)} %fusion.2) | data formatting | bytes 5308416 | tf_op jit(solution)/shard_map/concatenate | solution.py:106
  171.2 5.1 %maximum_bitcast_fusion = bf16[2,16,36,4608]{3,2,0,1:T(8,128)(2,1)S(1)} fusion(bf16[16,2,36,1152]{3,2,1,0:T(8,128)(2,1)S(1)} %convolution_convert_fusion.3, bf16[16,2,36,1152]{3,2,1,0:T(8,128)(2,1)S(1)} %concatenate.17, bf16[16,2,36,1152]{3,2,1,0:T(8,128)(2,1)} %concatenate.16, bf16[16,2,36,1152]{3,2,1,0:T(8,128)(2,1)} %concatenate.15), kind=kLoop, calls=%fused_computation.2 | loop fusion | flops 42467328 | bytes 21233664 | tf_op jit(solution)/shard_map/transpose | solution.py:33
  176.3 14.1 %copy.99 = bf16[2,16,36,4608]{3,1,0,2:T(8,128)(2,1)} copy(bf16[2,16,36,4608]{3,2,0,1:T(8,128)(2,1)S(1)} %maximum_bitcast_fusion) | data formatting | bytes 21233664 | tf_op jit(solution)/shard_map/transpose | solution.py:33
  190.4 30.6 %reduce-scatter.3.cloned.1.call-done = bf16[16,36,4608]{2,0,1:T(8,128)(2,1)} async-done(((bf16[32,36,4608]{2,0,1:T(8,128)(2,1)}), bf16[16,36,4608]{2,0,1:T(8,128)(2,1)}) %reduce-scatter.3.cloned.1.call-update) | async-done | bytes 5308432 | tf_op jit(solution)/shard_map/reduce_scatter | solution.py:34
  221.0 7.9 %copy.100 = bf16[16,36,4608]{2,1,0:T(8,128)(2,1)} copy(bf16[16,36,4608]{2,0,1:T(8,128)(2,1)} %reduce-scatter.3.cloned.1.call-done) | data formatting | bytes 10616832 | tf_op jit(solution)/shard_map/reduce_scatter | solution.py:34
  229.0 106.0 %reduce-scatter.5.cloned.1.call-done = bf16[1,36,4608]{2,1,0:T(8,128)(2,1)} async-done(((bf16[16,36,4608]{2,1,0:T(8,128)(2,1)}), bf16[1,36,4608]{2,1,0:T(8,128)(2,1)}) %reduce-scatter.5.cloned.1.call-update) | async-done | bytes 331792 | tf_op jit(solution)/shard_map/reduce_scatter | solution.py:35
  336.0 3.3 broadcast_in_dim.2
  339.3 4.8 %all-to-all-start = ((f32[8,36,4608]{2,1,0:T(8,128)}), f32[8,36,4608]{2,1,0:T(8,128)}, u32[]{:S(2)}, u32[]{:S(2)}) async-start(f32[8,36,4608]{2,1,0:T(8,128)} %broadcast_in_dim.2), calls=%async_computation.2 | async-start | bytes 11796480 | tf_op jit(solution)/shard_map/all_to_all | solution.py:40
  344.1 2.7 fusion.19
  346.9 2.7 convolution_add_fusion.1
  349.6 3.4 fusion.7
  353.0 57.1 %all-to-all-done = f32[8,36,4608]{2,1,0:T(8,128)} async-done(((f32[8,36,4608]{2,1,0:T(8,128)}), f32[8,36,4608]{2,1,0:T(8,128)}, u32[]{:S(2)}, u32[]{:S(2)}) %all-to-all-start) | async-done | bytes 5308448 | tf_op jit(solution)/shard_map/all_to_all | solution.py:40
  410.1 3.9 reduce_sum.29
  (49 shorter events, 25.5 us)
Async XLA Ops:
  7.2 108.6 %copy-start = (bf16[8,16,1152]{2,1,0:T(8,128)(2,1)S(1)}, bf16[8,16,1152]{2,1,0:T(8,128)(2,1)}, u32[]{:S(2)}) copy-start(bf16[8,16,1152]{2,1,0:T(8,128)(2,1)} %param.6) | copy-start | bytes 884740
  7.2 94.7 %all-gather.3.cloned.1.call-start = ((), (), s32[]{:S(2)}) async-start(), calls=%async_computation.5 | async-start | bytes 12165120 | tf_op jit(solution)/shard_map/all_gather | solution.py:21
  9.1 211.9 %reduce-scatter.3.cloned.1.call-start = ((), (), s32[]{:S(2)}) async-start(), calls=%async_computation.3 | async-start | bytes 15925248 | tf_op jit(solution)/shard_map/reduce_scatter | solution.py:34
  121.1 3.9 copy-start.7
  131.1 2.1 copy-start.5
  135.5 2.2 copy-start.6
  143.2 3.7 copy-start.2
  190.4 144.6 %reduce-scatter.5.cloned.1.call-start = ((), (), s32[]{:S(2)}) async-start(), calls=%async_computation.4 | async-start | bytes 6266880 | tf_op jit(solution)/shard_map/reduce_scatter | solution.py:35
  339.3 4.9 %copy-start.4 = (bf16[128,1152]{1,0:T(8,128)(2,1)S(1)}, bf16[128,1152]{1,0:T(8,128)(2,1)}, u32[]{:S(2)}) copy-start(bf16[128,1152]{1,0:T(8,128)(2,1)} %convert_element_type.94) | copy-start | bytes 884740
  339.3 70.8 %all-to-all-start = ((f32[8,36,4608]{2,1,0:T(8,128)}), f32[8,36,4608]{2,1,0:T(8,128)}, u32[]{:S(2)}, u32[]{:S(2)}) async-start(f32[8,36,4608]{2,1,0:T(8,128)} %broadcast_in_dim.2), calls=%async_computation.2 | async-start | bytes 11796480 | tf_op jit(solution)/shard_map/all_to_all | solution.py:40
  344.1 5.5 %copy-start.3 = (bf16[128,1152]{1,0:T(8,128)(2,1)S(1)}, bf16[128,1152]{1,0:T(8,128)(2,1)}, u32[]{:S(2)}) copy-start(bf16[128,1152]{1,0:T(8,128)(2,1)} %copy-done.2) | copy-start | bytes 884740
  346.9 67.2 %copy-start.1 = (bf16[8,16,1152]{2,1,0:T(8,128)(2,1)S(1)}, bf16[8,16,1152]{2,1,0:T(8,128)(2,1)}, u32[]{:S(2)}) copy-start(bf16[8,16,1152]{2,1,0:T(8,128)(2,1)} %param.6) | copy-start | bytes 884740
Sparse Core Ops, SparseCore 0:
  11.1 90.6 all-gather.2
  190.5 30.4 reduce-scatter.2
  229.1 105.8 reduce-scatter.4
where the time goes:
time: 423 us; the launch traced here: 421 us
  waiting for transfers between devices  286 us (68%)
  local copies, waits for them, and re-layouts  63 us (15%)
  matrix products  40.3 us (10%)
  between operations  14 us (3%)
  other arithmetic  11.9 us (3%)
  starting transfers between devices  4.97 us (1%)
    reduce_scatter x1, waiting for transfers between devices, sum_by_chip_2(): return lax.psum_scatter(pieces, chips, scatter_dimension=0, tiled=True)[0]  106 us
    all_gather x1, waiting for transfers between devices, side_by_side(): lax.all_gather(both, axis, axis=dim, tiled=True)  92.7 us
    all_to_all x1, waiting for transfers between devices, sent_to_all(): return lax.all_to_all(copies, axis, split_axis=0, concat_axis=0, tiled=True)  57.1 us
    reduce_scatter x1, waiting for transfers between devices, sum_by_chip_2(): pieces = lax.psum_scatter(pieces, core, scatter_dimension=0, tiled=True)  30.6 us
    transpose x1, local copies, waits for them, and re-layouts, sum_by_chip_2(): pieces = pieces.reshape(*sizes, *inside).swapaxes(0, 1).reshape(-1, *inside)  14.1 us
    unnamed x17, local copies, waits for them, and re-layouts  14 us
    concatenate x3, local copies, waits for them, and re-layouts, local(): jnp.concatenate([jnp.concatenate([contract_first(rows, dquery), contract_...  13.8 us
    dot_general x4, matrix products, contract_last(): lax.dot_general(left, right, (((1,), (1,)), ((), ())), preferred_element_...  11.4 us
  transfers between devices with their start and end apart: 4, of which 4 were waited for; matrix products, arithmetic and copies ran while one was open for 2% of the time, Pallas kernels for 0%

commit v1 on v0

v1 whole, which is shorter than its diff:
```python
import jax
import jax.numpy as jnp
from jax import lax
from jax.experimental import pallas as pl
from jax.experimental.pallas import tpu as pltpu
from jax.sharding import Mesh
from jax.sharding import PartitionSpec as P

D = 1152
FRAMES = 16
HEAD_DIM = 72
ZH, NX, NC, NY, ZL = 4, 4, 2, 4, 2
NZ = ZH * ZL
NPIX = ZH * NX * NC
NREP = NY * ZL
ROWS = 128
RP = D // NPIX
COLS = 2 * HEAD_DIM
RA = 128
RO = 48
RF = RA + RO
BF = jnp.bfloat16
F32 = jnp.float32
AXES = ("zh", "x", "c", "y", "zl")


def dot_nn(a, b):
    return lax.dot_general(a, b, (((1,), (0,)), ((), ())), preferred_element_type=F32)


def dot_nt(a, b):
    return lax.dot_general(a, b, (((1,), (1,)), ((), ())), preferred_element_type=F32)


def dot_tn(a, b):
    return lax.dot_general(a, b, (((0,), (0,)), ((), ())), preferred_element_type=F32)


def roll(v, shift):
    shift = shift % 128
    return v if shift == 0 else pltpu.roll(v, shift, 1)


def lanes(rows):
    return lax.broadcasted_iota(jnp.int32, (rows, 128), 1)


def kernel(
    x_ref, d_ref, wq_ref, wk_ref, wv_ref, wo_ref, gi_ref, gw_ref,
    XA, DA, WS, OSRC, WL, OL, WCAT, WOC, DQKV, AS, DXP, DXS, DXC, DXR,
    DWB, DWOB, DWS, RX, R2S, RZ, OS, OR, FL,
    lsem, a_s, a_r, w1s, w2s, w_r, o_s, o_r, xs_s, xs_r, xy_s, xy_r,
    r1_s, r1_r, r2_s, r2_r, ro_s, ro_r, f_s, f_r,
):
    zh, x, c, y, zl = [lax.axis_index(a) for a in AXES]
    pix = (zh * NX + x) * NC + c
    rep = y * ZL + zl
    z = zh * ZL + zl
    sib = 1 - c

    def rcopy(src, dst, ss, rs, dev):
        return pltpu.make_async_remote_copy(
            src_ref=src, dst_ref=dst, send_sem=ss, recv_sem=rs,
            device_id=dev, device_id_type=pl.DeviceIdType.MESH,
        )

    me = (zh, x, c, y, zl)
    acts = (XA, DA)

    def blk(kind, yb, cb):
        return acts[kind].at[yb, pl.ds(pl.multiple_of(cb * ROWS, ROWS), ROWS)]

    def act(kind, yb, cb, to_y, to_c, idx):
        return rcopy(
            blk(kind, yb, cb), blk(kind, yb, cb), a_s.at[idx],
            a_r.at[kind * 8 + yb * 2 + cb], (zh, x, to_c, to_y, zl),
        )

    own = [pltpu.make_async_copy(r, blk(k, y, c), lsem.at[k]) for k, r in enumerate((x_ref, d_ref))]
    for o in own:
        o.start()
    for o in own:
        o.wait()
    right, left, opp = (y + 1) % NY, (y + 3) % NY, (y + 2) % NY
    sends = [
        act(0, y, c, right, c, 0), act(1, y, c, left, c, 1),
        act(1, y, c, right, c, 2), act(0, y, c, left, c, 3),
        act(0, y, c, y, sib, 4), act(1, y, c, y, sib, 5),
    ]
    for s in sends:
        s.start()

    ii = lax.broadcasted_iota(jnp.int32, (D, 256), 0)
    nn = lax.broadcasted_iota(jnp.int32, (D, 256), 1)
    sel = jnp.where((ii == nn + COLS * rep) & (nn < COLS), 1.0, 0.0).astype(BF)
    tail = None
    for s, w in enumerate((wq_ref, wk_ref, wv_ref)):
        b = dot_nn(w[...], sel)
        WS[RP * s : RP * s + RP, :] = b[:, :128].astype(BF)
        t = b[:, 128:256]
        t = roll(t[: RP // 2], 32 * s) + roll(t[RP // 2 :], 32 * s + 16)
        tail = t if tail is None else tail + t
    WS[3 * RP : 3 * RP + RP // 2, :] = tail.astype(BF)
    want = jnp.where(nn < 128, nn + 128 * rep, nn - 128 + 1024 + 16 * rep)
    sel = jnp.where((ii == want) & (nn < COLS), 1.0, 0.0).astype(BF)
    b = dot_nn(wo_ref[...], sel)
    OSRC[:RP, :] = b[:, :128].astype(BF)
    t = b[:, 128:256]
    tail = t[:12] + roll(t[12:24], 16) + roll(t[24:36], 32)
    OSRC[RP : RP + 12, :] = tail.astype(BF)

    selfcore = zl == c

    @pl.when(selfcore)
    def _():
        WL[pix] = WS[...]

    def w1(i):
        zh2, zl2 = i // 2, i % 2
        return rcopy(WS, WL.at[pix], w1s.at[i], w_r.at[pix], (zh2, x, zl, y, zl2))

    def w1_not_self(i):
        return jnp.logical_not((i == z) & selfcore)

    @pl.loop(0, NZ)
    def _(i):
        @pl.when(w1_not_self(i))
        def _():
            w1(i).start()

    oslot = ((x % 2) * 2 + c) * NREP + rep
    oself = (zh == y) & (x // 2 == c)

    @pl.when(oself)
    def _():
        OL[oslot] = OSRC[...]

    def osend(i):
        dev = (i // 8, (i // 2) % 4, x // 2, zh, i % 2)
        return rcopy(OSRC, OL.at[oslot], o_s.at[i], o_r.at[oslot], dev)

    mine = (zh * NX + x) * ZL + zl

    def o_not_self(i):
        return jnp.logical_not((i == mine) & oself)

    @pl.loop(0, 32)
    def _(i):
        @pl.when(o_not_self(i))
        def _():
            osend(i).start()

    def w2(k, dx):
        p = ((k // 2) * NX + x) * NC + k % 2
        return rcopy(WL.at[p], WL.at[p], w2s.at[k * 3 + dx - 1], w_r.at[p], (zh, (x + dx) % NX, c, y, zl))

    def w_wait(p):
        rcopy(WL.at[p], WL.at[p], w2s.at[0], w_r.at[p], me).wait_recv()

    @pl.loop(0, 8)
    def _(k):
        p = ((k // 2) * NX + x) * NC + k % 2

        @pl.when(jnp.logical_not((p == pix) & selfcore))
        def _():
            w_wait(p)

        for dx in range(1, NX):
            w2(k, dx).start()

    def await_act(kind, yb, cb):
        act(kind, yb, cb, y, sib, 0).wait_recv()

    fwd = [
        act(0, left, c, right, c, 6), act(1, right, c, left, c, 7),
        act(0, left, c, y, sib, 8), act(1, right, c, y, sib, 9),
        act(1, left, c, y, sib, 10), act(0, right, c, y, sib, 11),
        act(0, opp, c, y, sib, 12), act(1, opp, c, y, sib, 13),
    ]
    await_act(0, left, c)
    fwd[0].start()
    fwd[2].start()
    await_act(1, right, c)
    fwd[1].start()
    fwd[3].start()
    await_act(1, left, c)
    fwd[4].start()
    await_act(0, right, c)
    fwd[5].start()
    await_act(0, opp, c)
    fwd[6].start()
    await_act(1, opp, c)
    fwd[7].start()

    @pl.loop(0, 24)
    def _(i):
        k, x2 = i % 8, (x + 1 + i // 8) % NX
        w_wait(((k // 2) * NX + x2) * NC + k % 2)

    @pl.loop(0, 32)
    def _(i):
        @pl.when(jnp.logical_not((i == oslot) & oself))
        def _():
            rcopy(OL.at[i], OL.at[i], o_s.at[0], o_r.at[i], me).wait_recv()

    low16 = lanes(RP // 2) < 16

    @pl.loop(0, 8)
    def _(g):
        out = WCAT.at[pl.ds(pl.multiple_of(g * 144, 16), 144)]
        for q in range(4):
            p = g * 4 + q
            base = RP * q
            tl = WL[p, 3 * RP : 3 * RP + RP // 2, :].astype(F32)
            for s in range(3):
                out[base : base + RP, 256 * s : 256 * s + 128] = WL[p, RP * s : RP * s + RP, :]
                for half in range(2):
                    v = jnp.where(low16, roll(tl, -(32 * s + 16 * half)), 0.0).astype(BF)
                    at = base + half * (RP // 2)
                    out[at : at + RP // 2, 256 * s + 128 : 256 * s + 256] = v

    WOC[COLS:, :] = jnp.zeros((256 - COLS, D), BF)
    lane12 = lanes(12)
    for q in range(4):
        parts = [None] * 3
        for r in range(NREP):
            WOC[RP * q : RP * q + RP, 128 * r : 128 * r + 128] = OL[q * NREP + r, :RP, :]
            tl = OL[q * NREP + r, RP : RP + 12, :].astype(F32)
            for t in range(3):
                v = jnp.where(lane12 // 16 == t, tl, 0.0)
                v = roll(v, 16 * (r - t))
                parts[t] = v if parts[t] is None else parts[t] + v
        for t in range(3):
            at = RP * q + 12 * t
            WOC[at : at + 12, 1024:1152] = parts[t].astype(BF)

    scale = 1.0 / HEAD_DIM**0.5
    row = lax.broadcasted_iota(jnp.int32, (ROWS, 128), 0)
    col = lax.broadcasted_iota(jnp.int32, (ROWS, 128), 1)
    inside = row // FRAMES == col // FRAMES
    lane256 = lax.broadcasted_iota(jnp.int32, (ROWS, 256), 1)
    first = lane256 < HEAD_DIM
    zero = jnp.zeros((ROWS, 256), BF)

    def two_heads(v):
        return jnp.concatenate([jnp.where(first, v, zero), jnp.where(first, zero, v)], axis=0)

    def dx_sib(i):
        return rcopy(
            DXP.at[i, pl.ds(pl.multiple_of(sib * ROWS, ROWS), ROWS)], DXS.at[i],
            xs_s.at[i], xs_r.at[i], (zh, x, sib, y, zl),
        )

    @pl.loop(0, NY)
    def _(off):
        i = (y + off) % NY

        @pl.when(off == 0)
        def _():
            await_act(0, y, sib)
            await_act(1, y, sib)

        @pl.when(off > 0)
        def _():
            await_act(0, i, sib)
            await_act(1, i, sib)

        qkv = dot_nn(XA[i], WCAT[...]).astype(BF)
        da = dot_nt(DA[i], WOC[...]).astype(BF)
        for h in range(2):
            rs = slice(h * ROWS, h * ROWS + ROWS)
            q, k, v, g = qkv[rs, :256], qkv[rs, 256:512], qkv[rs, 512:], da[rs]
            kk, vv = two_heads(k), two_heads(v)
            sc = dot_nt(q, kk) * scale
            dp = dot_nt(g, vv)
            probs, dscore = [], []
            for n in range(2):
                cs = slice(n * 128, n * 128 + 128)
                s1 = jnp.where(inside, sc[:, cs], -jnp.inf)
                e = jnp.exp(s1 - jnp.max(s1, axis=1, keepdims=True))
                p1 = e / jnp.sum(e, axis=1, keepdims=True)
                d1 = dp[:, cs]
                t1 = jnp.sum(d1 * p1, axis=1, keepdims=True)
                probs.append(p1.astype(BF))
                dscore.append((p1 * (d1 - t1) * scale).astype(BF))
            pb = jnp.concatenate(probs, axis=1)
            ds = jnp.concatenate(dscore, axis=1)
            AS[i, rs, :] = dot_nn(pb, vv).astype(BF)
            DQKV[i, rs, :256] = dot_nn(ds, kk).astype(BF)
            dk = dot_tn(ds, q)
            DQKV[i, rs, 256:512] = jnp.where(first, dk[:128], dk[128:]).astype(BF)
            dv = dot_tn(pb, g)
            DQKV[i, rs, 512:] = jnp.where(first, dv[:128], dv[128:]).astype(BF)
        DXP[i] = dot_nt(DQKV[i], WCAT[...]).astype(BF)
        dx_sib(i).start()

    dq_all = DQKV[...].reshape(NY * 256, 768)

    @pl.loop(0, 9)
    def _(i):
        at = pl.multiple_of(i * 128, 128)
        lhs = XA[:, :, pl.ds(at, 128)].reshape(NY * 256, 128)
        DWB[pl.ds(at, 128), :] = dot_tn(lhs, dq_all).astype(BF)

    @pl.loop(0, 8)
    def _(g):
        src = DWB.at[pl.ds(pl.multiple_of(g * 144, 16), 144)]
        for q in range(4):
            p = g * 4 + q
            x2, k = (p // 2) % NX, (p // 8) * 2 + p % 2
            base = RP * q
            tail = None
            for s in range(3):
                DWS[x2, k, RP * s : RP * s + RP, :] = src[base : base + RP, 256 * s : 256 * s + 128]
                t = src[base : base + RP, 256 * s + 128 : 256 * s + 256].astype(F32)
                t = roll(t[: RP // 2], 32 * s) + roll(t[RP // 2 :], 32 * s + 16)
                tail = t if tail is None else tail + t
            DWS[x2, k, 3 * RP : 3 * RP + RP // 2, :] = tail.astype(BF)

    def r1(dx):
        x2 = (x + dx) % NX
        return rcopy(DWS.at[x2], RX.at[x], r1_s.at[dx - 1], r1_r.at[x], (zh, x2, c, y, zl))

    for dx in range(1, NX):
        r1(dx).start()

    DWOB[...] = dot_tn(AS[...].reshape(NY * 256, 256), DA[...].reshape(NY * 256, D)).astype(BF)
    for q in range(4):
        tt = [DWOB[RP * q + 12 * t : RP * q + 12 * t + 12, 1024:1152].astype(F32) for t in range(3)]
        for r in range(NREP):
            OS[q * NREP + r, :RP, :] = DWOB[RP * q : RP * q + RP, 128 * r : 128 * r + 128]
            tail = None
            for t in range(3):
                v = roll(jnp.where(lane12 // 16 == r, tt[t], 0.0), 16 * (t - r))
                tail = v if tail is None else tail + v
            OS[q * NREP + r, RP : RP + 12, :] = tail.astype(BF)

    def ro(i):
        q, r = i // NREP, i % NREP
        dev = (y, 2 * c + q // 2, q % 2, r // ZL, r % ZL)
        return rcopy(OS.at[i], OR.at[mine], ro_s.at[i], ro_r.at[mine], dev)

    def ro_not_self(i):
        return jnp.logical_not((i == oslot) & oself)

    @pl.loop(0, 32)
    def _(i):
        @pl.when(ro_not_self(i))
        def _():
            ro(i).start()

    @pl.when(oself)
    def _():
        OR[mine] = OS[oslot]

    def dx_y(dy):
        i = (y + dy) % NY
        return rcopy(DXC.at[i], DXR.at[dy - 1], xy_s.at[dy - 1], xy_r.at[dy - 1], (zh, x, c, i, zl))

    for dy in (1, 3, 2, 0):
        i = (y + dy) % NY
        dx_sib(i).wait_recv()
        both = DXP[i, pl.ds(pl.multiple_of(c * ROWS, ROWS), ROWS), :].astype(F32) + DXS[i].astype(F32)
        if dy:
            DXC[i] = both.astype(BF)
            dx_y(dy).start()

    for dx in range(1, NX):
        x2 = (x + dx) % NX
        rcopy(RX.at[x2], RX.at[x2], r1_s.at[0], r1_r.at[x2], me).wait_recv()

    def r2(k):
        return rcopy(R2S.at[k], RZ.at[z], r2_s.at[k], r2_r.at[z], (k // 2, x, k % 2, y, c))

    kown = zh * 2 + c

    @pl.loop(0, 8)
    def _(k):
        acc = DWS[x, k].astype(F32)
        for dx in range(1, NX):
            acc = acc + RX[(x + dx) % NX, k].astype(F32)
        R2S[k] = acc.astype(BF)

        @pl.when(jnp.logical_not((k == kown) & selfcore))
        def _():
            r2(k).start()

    @pl.when(selfcore)
    def _():
        RZ[z] = R2S[kown]

    for dy in range(1, NY):
        dx_y(dy).wait_recv()
    both = both + DXR[0].astype(F32) + DXR[1].astype(F32) + DXR[2].astype(F32)
    gi_ref[...] = both.astype(BF)

    @pl.loop(0, 32)
    def _(i):
        @pl.when(jnp.logical_not((i == mine) & oself))
        def _():
            rcopy(OR.at[i], OR.at[i], ro_s.at[0], ro_r.at[i], me).wait_recv()

    osum = OR[0].astype(F32)
    for i in range(1, 32):
        osum = osum + OR[i].astype(F32)
    FL[rep, RA:, :] = osum.astype(BF)

    @pl.loop(0, NZ)
    def _(i):
        @pl.when(jnp.logical_not((i == z) & selfcore))
        def _():
            rcopy(RZ.at[i], RZ.at[i], r2_s.at[0], r2_r.at[i], me).wait_recv()

    asum = RZ[0].astype(F32)
    for i in range(1, NZ):
        asum = asum + RZ[i].astype(F32)
    FL[rep, :RA, :] = asum.astype(BF)

    def fin(dr):
        r = (rep + dr) % NREP
        return rcopy(FL.at[rep], FL.at[rep], f_s.at[dr - 1], f_r.at[rep], (zh, x, c, r // ZL, r % ZL))

    @pl.loop(1, NREP)
    def _(dr):
        fin(dr).start()

    for i, s in enumerate(sends + fwd):
        s.wait_send()

    @pl.loop(0, NZ)
    def _(i):
        @pl.when(w1_not_self(i))
        def _():
            w1(i).wait_send()

    @pl.loop(0, 32)
    def _(i):
        @pl.when(o_not_self(i))
        def _():
            osend(i).wait_send()

        @pl.when(ro_not_self(i))
        def _():
            ro(i).wait_send()

    @pl.loop(0, 8)
    def _(k):
        for dx in range(1, NX):
            w2(k, dx).wait_send()

        @pl.when(jnp.logical_not((k == kown) & selfcore))
        def _():
            r2(k).wait_send()

    for i in range(NY):
        dx_sib(i).wait_send()
    for dy in range(1, NY):
        dx_y(dy).wait_send()
    for dx in range(1, NX):
        r1(dx).wait_send()

    @pl.loop(1, NREP)
    def _(dr):
        r = (rep + dr) % NREP
        rcopy(FL.at[r], FL.at[r], f_s.at[0], f_r.at[r], me).wait_recv()
        fin(dr).wait_send()

    lane36 = lanes(RP)
    for s in range(3):
        last, lastt = None, None
        for t in range(9):
            if t < 8:
                main = roll(FL[t, RP * s : RP * s + RP, :].astype(F32), 16 * t)
            out = main
            if t > 0:
                prev = jnp.where(lane36 < 16 * (t - 1), last, lastt)
                out = prev if t == 8 else jnp.where(lane36 >= 16 * t, main, prev)
            gw_ref[:, s * D + 128 * t : s * D + 128 * t + 128] = out
            if t < 8:
                last = main
                tl = FL[t, 3 * RP : 3 * RP + RP // 2, :].astype(F32)
                halves = [roll(tl, 16 * t - 32 * s - 16 * h) for h in range(2)]
                lastt = jnp.concatenate(halves, axis=0)
    parts = [None] * 3
    for r in range(NREP):
        gw_ref[:, 3 * D + 128 * r : 3 * D + 128 * r + 128] = FL[r, RA : RA + RP, :].astype(F32)
        tl = FL[r, RA + RP : RA + RP + 12, :].astype(F32)
        for t in range(3):
            v = roll(jnp.where(lane12 // 16 == t, tl, 0.0), 16 * (r - t))
            parts[t] = v if parts[t] is None else parts[t] + v
    gw_ref[:, 3 * D + 1024 :] = jnp.concatenate(parts, axis=0)


def vm(*shape, dtype=BF):
    return pltpu.VMEM(shape, dtype)


def local(tokens, out_grad, wq, wk, wv, wo):
    rows = tokens.reshape(-1, D)
    drows = out_grad.reshape(-1, D)
    dma = lambda n: pltpu.SemaphoreType.DMA((n,))
    vmem = pl.BlockSpec(memory_space=pltpu.VMEM)
    hbm = pl.BlockSpec(memory_space=pl.ANY)
    gi, gw = pl.pallas_call(
        kernel,
        out_shape=(
            jax.ShapeDtypeStruct((ROWS, D), BF),
            jax.ShapeDtypeStruct((RP, 4 * D), F32),
        ),
        in_specs=[hbm, hbm, vmem, vmem, vmem, vmem],
        out_specs=(vmem, vmem),
        scratch_shapes=[
            vm(NY, 256, D), vm(NY, 256, D),
            vm(RA, 128), vm(RO, 128), vm(NPIX, RA, 128), vm(32, RO, 128),
            vm(D, 768), vm(256, D), vm(NY, 256, 768), vm(NY, 256, 256),
            vm(NY, 256, D), vm(NY, ROWS, D), vm(NY, ROWS, D), vm(3, ROWS, D),
            vm(D, 768), vm(256, D), vm(NX, 8, RA, 128), vm(NX, 8, RA, 128),
            vm(8, RA, 128), vm(NZ, RA, 128), vm(32, RO, 128), vm(32, RO, 128),
            vm(NREP, RF, 128),
            dma(2), dma(14), dma(16), dma(8), dma(24), dma(32), dma(32), dma(32),
            dma(4), dma(4), dma(3), dma(3), dma(3), dma(4), dma(8), dma(8),
            dma(32), dma(32), dma(7), dma(8),
        ],
        compiler_params=pltpu.CompilerParams(has_side_effects=True, vmem_limit_bytes=60 * 2**20),
    )(rows, drows, wq, wk, wv, wo)
    return gi.reshape(tokens.shape), gw


def solution(mesh):
    torus = Mesh(mesh.devices.reshape(ZH, NX, NC, NY, ZL), AXES)
    act = P(AXES, None, None)
    w = P(("zh", "x", "c"), None)
    return jax.shard_map(
        local,
        mesh=torus,
        in_specs=(act, act, w, w, w, w),
        out_specs=(act, w),
        check_vma=False,
    )
```

time: 423 us -> 112 us (0.26)
  waiting for transfers between devices: 286 us -> 0 us
  Pallas kernels: 0 us -> 107 us
  local copies, waits for them, and re-layouts: 63 us -> 3.72 us
  matrix products: 40.3 us -> 0 us
  between operations: 14 us -> 0.64 us
  other arithmetic: 11.9 us -> 0 us
  starting transfers between devices: 4.97 us -> 0 us
    reduce_scatter x2 -> x0, waiting for transfers between devices: 137 us -> none  [the longest x1 106 us: sum_by_chip_2(): return lax.psum_scatter(pieces, chips, scatter_dimension=0, tiled=True)[0]]
    pallas_call x0 -> x1, Pallas kernels: none -> 107 us  [local(): pl.pallas_call(kernel, out_shape=(jax.ShapeDtypeStruct((ROWS, D), BF), ja...]
    all_gather x1 -> x0, waiting for transfers between devices: 92.7 us -> none  [side_by_side(): lax.all_gather(both, axis, axis=dim, tiled=True)]
    all_to_all x1 -> x0, waiting for transfers between devices: 57.1 us -> none  [sent_to_all(): return lax.all_to_all(copies, axis, split_axis=0, concat_axis=0, tiled=True)]
    dot_general x16 -> x0, matrix products: 38.6 us -> none  [the longest x4 11.4 us: contract_last(): lax.dot_general(left, right, (((1,), (1,)), ((), ())), preferred_element_...]
    transpose x1 -> x0, local copies, waits for them, and re-layouts: 14.1 us -> none  [sum_by_chip_2(): pieces = pieces.reshape(*sizes, *inside).swapaxes(0, 1).reshape(-1, *inside)]
    concatenate x3 -> x0, local copies, waits for them, and re-layouts: 13.8 us -> none  [local(): jnp.concatenate([jnp.concatenate([contract_first(rows, dquery), contract_...]
    unnamed x17 -> x2, local copies, waits for them, and re-layouts: 14 us -> 3.72 us
  transfers between devices with their start and end apart: 4 -> 0, of which waited for: 4 -> 0; matrix products, arithmetic and copies ran while one was open for 2% -> 0% of each run, Pallas kernels for 0% -> 0%
where the time goes in v1:
time: 112 us; the launch traced here: 111 us
  Pallas kernels  107 us (96%)
  local copies, waits for them, and re-layouts  3.72 us (3%)
    pallas_call x1, Pallas kernels, local(): pl.pallas_call(kernel, out_shape=(jax.ShapeDtypeStruct((ROWS, D), BF), ja...  107 us
    unnamed x2, local copies, waits for them, and re-layouts  3.72 us

profile of v1, /device:TPU:1, one launch (start us, length us, event | category | flops | bytes accessed | tf_op | source)
XLA Modules:
  0.0 110.9 jit_solution(14733652464144150975)
XLA Ops:
  0.6 106.6 %shard_map.77 = (bf16[128,1152]{1,0:T(8,128)(2,1)}, f32[36,4608]{1,0:T(8,128)}) custom-call(bf16[128,1152]{1,0:T(8,128)(2,1)} %bitcast.4, bf16[128,1152]{1,0:T(8,128)(2,1)} %bitcast.5, bf16[36,1152]{1,0:T(8,128)(2,1)} %wq_ref.1, bf16[36,1152]{1,0:T(8,128)(2,1)} %wk_ref.1, bf16[36,1152]{1,0:T(8,128)(2,1)} %wv_ref.1, bf16[36,1152]{1,0:T(8,128)(2,1)} %wo_ref.1), custom_call_target="tpu_custom_call" | custom-call | tf_op jit(solution)/shard_map/pallas_call | solution.py:504
  107.2 1.7 %copy.10 = bf16[8,16,1152]{2,1,0:T(8,128)(2,1)} copy(bf16[8,16,1152]{2,1,0:T(8,128)(2,1)} %bitcast.3) | data formatting | bytes 589824
  108.9 2.0 %copy.11 = f32[36,4608]{1,0:T(8,128)} copy(f32[36,4608]{1,0:T(8,128)} %get-tuple-element.9) | data formatting | bytes 1327104

commit v2 on v1

v2 whole, which is shorter than its diff:
```python
import jax
import jax.numpy as jnp
from jax import lax
from jax.experimental import pallas as pl
from jax.experimental.pallas import tpu as pltpu
from jax.sharding import Mesh
from jax.sharding import PartitionSpec as P

D = 1152
FRAMES = 16
HEAD_DIM = 72
ZH, NX, NC, NY, ZL = 4, 4, 2, 4, 2
NZ = ZH * ZL
NPIX = ZH * NX * NC
NREP = NY * ZL
ROWS = 128
RP = D // NPIX
COLS = 2 * HEAD_DIM
RA = 128
RO = 48
RF = RA + RO
BF = jnp.bfloat16
F32 = jnp.float32
AXES = ("zh", "x", "c", "y", "zl")


def dot_nn(a, b):
    return lax.dot_general(a, b, (((1,), (0,)), ((), ())), preferred_element_type=F32)


def dot_nt(a, b):
    return lax.dot_general(a, b, (((1,), (1,)), ((), ())), preferred_element_type=F32)


def dot_tn(a, b):
    return lax.dot_general(a, b, (((0,), (0,)), ((), ())), preferred_element_type=F32)


def roll(v, shift):
    shift = shift % 128
    return v if shift == 0 else pltpu.roll(v, shift, 1)


def lanes(rows):
    return lax.broadcasted_iota(jnp.int32, (rows, 128), 1)


def kernel(
    x_ref, d_ref, wq_ref, wk_ref, wv_ref, wo_ref, gi_ref, gw_ref,
    XA, DA, WIN, WS, OSRC, OH, WL, OL, WCAT, WOC, DQKV, AS, DXP, DXS, DXC, DXH, DXR,
    DWB, DWOB, DWS, RXA, SMB, RL, RR, R2S, RZ, FO, FL,
    lsem, a_s, a_r, h_s, h_r, w1s, w2s, w_r, o1s, o2s, o_r, xs_s, xs_r, xh_s, xh_r, xy_s, xy_r,
    a2_s, a2_r, im_s, im_r, sm_s, sm_r, r2_s, r2_r, t_s, t_r, fa_s, fa_r, fo_s, fo_r,
):
    zh, x, c, y, zl = [lax.axis_index(a) for a in AXES]
    pix = (zh * NX + x) * NC + c
    rep = y * ZL + zl
    z = zh * ZL + zl
    sib = 1 - c
    me = (zh, x, c, y, zl)
    selfcore = zl == c
    right, left, opp = (y + 1) % NY, (y + 3) % NY, (y + 2) % NY
    xr, xl, xo = (x + 1) % NX, (x + 3) % NX, (x + 2) % NX
    hub = (y, (x % 2) * 2 + zl, c, zh, x // 2)
    home = (y, 2 * zl + x // 2, c, zh, x % 2)
    hub_self = (y == zh) & ((x % 2) * 2 + zl == x) & (zl == x // 2)
    hub_other = jnp.logical_not(hub_self)

    def rcopy(src, dst, ss, rs, dev):
        return pltpu.make_async_remote_copy(
            src_ref=src, dst_ref=dst, send_sem=ss, recv_sem=rs,
            device_id=dev, device_id_type=pl.DeviceIdType.MESH,
        )

    def blk(kind, yb, cb):
        return (XA, DA)[kind].at[yb, pl.ds(pl.multiple_of(cb * ROWS, ROWS), ROWS)]

    wins = [
        pltpu.make_async_copy(r, WIN.at[k], lsem.at[2 + k])
        for k, r in enumerate((wq_ref, wk_ref, wv_ref, wo_ref))
    ]
    own = [pltpu.make_async_copy(r, blk(k, y, c), lsem.at[k]) for k, r in enumerate((x_ref, d_ref))]
    for o in own + wins:
        o.start()
    bar = pltpu.get_barrier_semaphore()

    def greet(dev):
        pl.semaphore_signal(bar, inc=1, device_id=dev, device_id_type=pl.DeviceIdType.MESH)

    @pl.loop(0, 16)
    def _(i):
        @pl.when(i != z * 2 + c)
        def _():
            greet((i // 4, x, i % 2, y, (i // 2) % 2))

    for dy in range(1, NY):
        greet((zh, x, c, (y + dy) % NY, zl))
        greet((zh, x, c, (y + dy) % NY, 1 - zl))
    greet((zh, xr, c, y, zl))
    greet((zh, xl, c, y, zl))

    @pl.when(hub_other)
    def _():
        greet(hub)
        greet(home)

    ii = lax.broadcasted_iota(jnp.int32, (D, 256), 0)
    nn = lax.broadcasted_iota(jnp.int32, (D, 256), 1)
    sel = jnp.where((ii == nn + COLS * rep) & (nn < COLS), 1.0, 0.0).astype(BF)
    want = jnp.where(nn < 128, nn + 128 * rep, nn - 128 + 1024 + 16 * rep)
    osel = jnp.where((ii == want) & (nn < COLS), 1.0, 0.0).astype(BF)
    for w in wins:
        w.wait()
    tail = None
    for s in range(3):
        b = dot_nn(WIN[s], sel)
        WS[RP * s : RP * s + RP, :] = b[:, :128].astype(BF)
        t = b[:, 128:256]
        t = roll(t[: RP // 2], 32 * s) + roll(t[RP // 2 :], 32 * s + 16)
        tail = t if tail is None else tail + t
    WS[3 * RP : 3 * RP + RP // 2, :] = tail.astype(BF)
    b = dot_nn(WIN[3], osel)
    OSRC[:RP, :] = b[:, :128].astype(BF)
    t = b[:, 128:256]
    tail = t[:12] + roll(t[12:24], 16) + roll(t[24:36], 32)
    OSRC[RP : RP + 12, :] = tail.astype(BF)
    for o in own:
        o.wait()

    @pl.when(hub_self)
    def _():
        pl.semaphore_wait(bar, 15 + 6 + 2)

    @pl.when(hub_other)
    def _():
        pl.semaphore_wait(bar, 15 + 6 + 2 + 2)

    def act(kind, yb, cb, to_y, to_c, idx):
        return rcopy(
            blk(kind, yb, cb), blk(kind, yb, cb), a_s.at[idx],
            a_r.at[kind * 8 + yb * 2 + cb], (zh, x, to_c, to_y, zl),
        )

    def hub_copy():
        return rcopy(OSRC, OH, h_s.at[0], h_r.at[0], hub)

    sends = [
        act(0, y, c, right, c, 0), act(1, y, c, left, c, 1),
        act(1, y, c, right, c, 2), act(0, y, c, left, c, 3),
        act(0, y, c, y, sib, 4), act(1, y, c, y, sib, 5),
    ]

    @pl.when(hub_other)
    def _():
        hub_copy().start()

    for s in sends[:4]:
        s.start()

    def col(k, xs):
        return ((k // 2) * NX + xs) * NC + k % 2

    def along_z(src, buf, ss, rs, i):
        return rcopy(src, buf.at[pix], ss.at[i], rs.at[pix], (i // 2, x, zl, y, i % 2))

    def not_self(i):
        return jnp.logical_not((i == z) & selfcore)

    def spread(src, buf, ss, rs):
        @pl.when(selfcore)
        def _():
            buf[pix] = src[...]

        @pl.loop(0, NZ)
        def _(i):
            @pl.when(not_self(i))
            def _():
                along_z(src, buf, ss, rs, i).start()

    def around_x(buf, ss, rs, p, to, idx):
        return rcopy(buf.at[p], buf.at[p], ss.at[idx], rs.at[p], (zh, to, c, y, zl))

    def arrived(buf, rs, p):
        rcopy(buf.at[p], buf.at[p], w1s.at[0], rs.at[p], me).wait_recv()

    def both_ways(buf, ss, rs):
        @pl.loop(0, 8)
        def _(k):
            p = col(k, x)

            @pl.when(jnp.logical_not((p == pix) & selfcore))
            def _():
                arrived(buf, rs, p)

            around_x(buf, ss, rs, p, xr, k).start()
            around_x(buf, ss, rs, p, xl, 8 + k).start()

    def onward(buf, ss, rs):
        @pl.loop(0, 4)
        def _(k):
            p, q = col(k, xl), col(k + 4, xr)
            arrived(buf, rs, p)
            around_x(buf, ss, rs, p, xr, 16 + k).start()
            arrived(buf, rs, q)
            around_x(buf, ss, rs, q, xl, 20 + k).start()

    def rest(buf, rs):
        @pl.loop(0, 4)
        def _(k):
            arrived(buf, rs, col(k + 4, xl))
            arrived(buf, rs, col(k, xr))
            arrived(buf, rs, col(k, xo))
            arrived(buf, rs, col(k + 4, xo))

    spread(WS, WL, w1s, w_r)
    for s in sends[4:]:
        s.start()

    @pl.when(hub_other)
    def _():
        hub_copy().wait_recv()

    @pl.when(hub_self)
    def _():
        OH[...] = OSRC[...]

    spread(OH, OL, o1s, o_r)
    both_ways(WL, w2s, w_r)
    both_ways(OL, o2s, o_r)

    def await_act(kind, yb, cb):
        act(kind, yb, cb, y, sib, 0).wait_recv()

    fwd = [
        act(0, left, c, right, c, 6), act(1, right, c, left, c, 7),
        act(0, left, c, y, sib, 8), act(1, right, c, y, sib, 9),
        act(1, left, c, y, sib, 10), act(0, right, c, y, sib, 11),
        act(0, opp, c, y, sib, 12), act(1, opp, c, y, sib, 13),
    ]
    await_act(0, left, c)
    fwd[0].start()
    fwd[2].start()
    await_act(1, right, c)
    fwd[1].start()
    fwd[3].start()
    onward(WL, w2s, w_r)
    onward(OL, o2s, o_r)
    rest(WL, w_r)
    rest(OL, o_r)

    low16 = lanes(RP // 2) < 16

    @pl.loop(0, 8)
    def _(g):
        out = WCAT.at[pl.ds(pl.multiple_of(g * 144, 16), 144)]
        for q in range(4):
            p = g * 4 + q
            base = RP * q
            tl = WL[p, 3 * RP : 3 * RP + RP // 2, :].astype(F32)
            for s in range(3):
                out[base : base + RP, 256 * s : 256 * s + 128] = WL[p, RP * s : RP * s + RP, :]
                for half in range(2):
                    v = jnp.where(low16, roll(tl, -(32 * s + 16 * half)), 0.0).astype(BF)
                    at = base + half * (RP // 2)
                    out[at : at + RP // 2, 256 * s + 128 : 256 * s + 256] = v

    def oslot(q, r):
        return ((r // 2) * NX + (q // 2) * 2 + r % 2) * NC + q % 2

    WOC[COLS:, :] = jnp.zeros((256 - COLS, D), BF)
    lane12 = lanes(12)
    for q in range(4):
        parts = [None] * 3
        for r in range(NREP):
            WOC[RP * q : RP * q + RP, 128 * r : 128 * r + 128] = OL[oslot(q, r), :RP, :]
            tl = OL[oslot(q, r), RP : RP + 12, :].astype(F32)
            for t in range(3):
                v = jnp.where(lane12 // 16 == t, tl, 0.0)
                v = roll(v, 16 * (r - t))
                parts[t] = v if parts[t] is None else parts[t] + v
        for t in range(3):
            at = RP * q + 12 * t
            WOC[at : at + 12, 1024:1152] = parts[t].astype(BF)

    await_act(1, left, c)
    fwd[4].start()
    await_act(0, right, c)
    fwd[5].start()

    scale = 1.0 / HEAD_DIM**0.5
    row = lax.broadcasted_iota(jnp.int32, (ROWS, 128), 0)
    col_ = lax.broadcasted_iota(jnp.int32, (ROWS, 128), 1)
    inside = row // FRAMES == col_ // FRAMES
    lane256 = lax.broadcasted_iota(jnp.int32, (ROWS, 256), 1)
    first = lane256 < HEAD_DIM
    zero = jnp.zeros((ROWS, 256), BF)

    def two_heads(v):
        return jnp.concatenate([jnp.where(first, v, zero), jnp.where(first, zero, v)], axis=0)

    def dx_sib(i):
        return rcopy(
            DXP.at[i, pl.ds(pl.multiple_of(sib * ROWS, ROWS), ROWS)], DXS.at[i],
            xs_s.at[i], xs_r.at[i], (zh, x, sib, y, zl),
        )

    @pl.loop(0, NY)
    def _(n):
        off = jnp.where(n == 1, 3, jnp.where(n == 2, 1, jnp.where(n == 3, 2, 0)))
        i = (y + off) % NY

        @pl.when(n == 3)
        def _():
            await_act(0, opp, c)
            fwd[6].start()
            await_act(1, opp, c)
            fwd[7].start()

        await_act(0, i, sib)
        await_act(1, i, sib)
        qkv = dot_nn(XA[i], WCAT[...]).astype(BF)
        da = dot_nt(DA[i], WOC[...]).astype(BF)
        for h in range(2):
            rs = slice(h * ROWS, h * ROWS + ROWS)
            q, k, v, g = qkv[rs, :256], qkv[rs, 256:512], qkv[rs, 512:], da[rs]
            kk, vv = two_heads(k), two_heads(v)
            sc = dot_nt(q, kk) * scale
            dp = dot_nt(g, vv)
            probs, dscore = [], []
            for n2 in range(2):
                cs = slice(n2 * 128, n2 * 128 + 128)
                s1 = jnp.where(inside, sc[:, cs], -jnp.inf)
                e = jnp.exp(s1 - jnp.max(s1, axis=1, keepdims=True))
                p1 = e / jnp.sum(e, axis=1, keepdims=True)
                d1 = dp[:, cs]
                t1 = jnp.sum(d1 * p1, axis=1, keepdims=True)
                probs.append(p1.astype(BF))
                dscore.append((p1 * (d1 - t1) * scale).astype(BF))
            pb = jnp.concatenate(probs, axis=1)
            ds = jnp.concatenate(dscore, axis=1)
            AS[i, rs, :] = dot_nn(pb, vv).astype(BF)
            DQKV[i, rs, :256] = dot_nn(ds, kk).astype(BF)
            dk = dot_tn(ds, q)
            DQKV[i, rs, 256:512] = jnp.where(first, dk[:128], dk[128:]).astype(BF)
            dv = dot_tn(pb, g)
            DQKV[i, rs, 512:] = jnp.where(first, dv[:128], dv[128:]).astype(BF)
        DXP[i] = dot_nt(DQKV[i], WCAT[...]).astype(BF)
        dx_sib(i).start()

    dq_all = DQKV[...].reshape(NY * 256, 768)

    @pl.loop(0, 9)
    def _(i):
        at = pl.multiple_of(i * 128, 128)
        lhs = XA[:, :, pl.ds(at, 128)].reshape(NY * 256, 128)
        DWB[pl.ds(at, 128), :] = dot_tn(lhs, dq_all).astype(BF)

    DWOB[...] = dot_tn(AS[...].reshape(NY * 256, 256), DA[...].reshape(NY * 256, D)).astype(BF)

    @pl.loop(0, 8)
    def _(g):
        src = DWB.at[pl.ds(pl.multiple_of(g * 144, 16), 144)]
        for q in range(4):
            p = g * 4 + q
            x2, k = (p // 2) % NX, (p // 8) * 2 + p % 2
            base = RP * q
            tail = None
            for s in range(3):
                DWS[x2, k, RP * s : RP * s + RP, :] = src[base : base + RP, 256 * s : 256 * s + 128]
                t = src[base : base + RP, 256 * s + 128 : 256 * s + 256].astype(F32)
                t = roll(t[: RP // 2], 32 * s) + roll(t[RP // 2 :], 32 * s + 16)
                tail = t if tail is None else tail + t
            DWS[x2, k, 3 * RP : 3 * RP + RP // 2, :] = tail.astype(BF)

    for q in range(4):
        tt = [DWOB[RP * q + 12 * t : RP * q + 12 * t + 12, 1024:1152].astype(F32) for t in range(3)]
        for r in range(NREP):
            p = oslot(q, r)
            x2, k = (p // 2) % NX, (p // 8) * 2 + p % 2
            DWS[x2, k, RA : RA + RP, :] = DWOB[RP * q : RP * q + RP, 128 * r : 128 * r + 128]
            tail = None
            for t in range(3):
                v = roll(jnp.where(lane12 // 16 == r, tt[t], 0.0), 16 * (t - r))
                tail = v if tail is None else tail + v
            DWS[x2, k, RA + RP : RF, :] = tail.astype(BF)

    def two(k):
        return pl.ds(k, 2)

    def to_x(src, dst, ss, rs, h, side):
        return rcopy(src, dst, ss.at[h * 2 + side], rs.at[h * 2 + side], (zh, (xr, xl)[side], c, y, zl))

    def far(h, side):
        ks = two((2 * h, 4 + 2 * h)[side])
        return to_x(DWS.at[xo, ks], RXA.at[ks], a2_s, a2_r, h, side)

    def near(h, side):
        ks = two((4 + 2 * h, 2 * h)[side])
        return to_x(DWS.at[(xr, xl)[side], ks], (RL, RR)[side].at[ks], im_s, im_r, h, side)

    def summed(h, side):
        ks = two((2 * h, 4 + 2 * h)[side])
        return to_x(SMB.at[ks], (RL, RR)[side].at[ks], sm_s, sm_r, h, side)

    def add_far(h):
        for side in range(2):
            far(h, side).wait_recv()
            k0 = (2 * h, 4 + 2 * h)[side]
            for k in (k0, k0 + 1):
                t = DWS[(xr, xl)[side], k].astype(F32) + RXA[k].astype(F32)
                SMB[k] = t.astype(BF)
            summed(h, side).start()

    for side in range(2):
        far(0, side).start()
    for side in range(2):
        near(0, side).start()
    for side in range(2):
        far(1, side).start()

    def own_sum(i):
        half = pl.ds(pl.multiple_of(c * ROWS, ROWS), ROWS)
        return DXP[i, half, :].astype(F32) + DXS[i].astype(F32)

    def dx_far(side):
        rows = pl.ds(64 * side, 64)
        return rcopy(
            DXC.at[0, rows], DXH.at[side], xh_s.at[side], xh_r.at[side],
            (zh, x, c, (right, left)[side], zl),
        )

    def dx_near(side):
        return rcopy(
            DXC.at[1 + side], DXR.at[side], xy_s.at[side], xy_r.at[side],
            (zh, x, c, (right, left)[side], zl),
        )

    for i in range(NY):
        dx_sib(i).wait_recv()
    DXC[0] = own_sum(opp).astype(BF)
    for side in range(2):
        dx_far(side).start()

    add_far(0)
    for side in range(2):
        near(1, side).start()
    for side in range(2):
        dx_far(side).wait_recv()
        t = own_sum((right, left)[side])
        a, b = t[:64], t[64:]
        if side == 0:
            a = a + DXH[0].astype(F32)
        else:
            b = b + DXH[1].astype(F32)
        DXC[1 + side, :64, :] = a.astype(BF)
        DXC[1 + side, 64:, :] = b.astype(BF)
        dx_near(side).start()
    add_far(1)

    def r2(k):
        return rcopy(R2S.at[k], RZ.at[z], r2_s.at[k], r2_r.at[z], (k // 2, x, k % 2, y, c))

    kown = zh * 2 + c

    def k_not_self(k):
        return jnp.logical_not((k == kown) & selfcore)

    for h in range(2):
        for side in range(2):
            near(h, side).wait_recv()
            summed(h, side).wait_recv()
        for k in (2 * h, 2 * h + 1, 4 + 2 * h, 5 + 2 * h):
            t = DWS[x, k].astype(F32) + RL[k].astype(F32) + RR[k].astype(F32)
            R2S[k] = t.astype(BF)

            @pl.when(k_not_self(k))
            def _():
                r2(k).start()

    @pl.when(selfcore)
    def _():
        RZ[z] = R2S[kown]

    for side in range(2):
        dx_near(side).wait_recv()
    gi_ref[...] = (own_sum(y) + DXR[0].astype(F32) + DXR[1].astype(F32)).astype(BF)

    @pl.loop(0, NZ)
    def _(i):
        @pl.when(not_self(i))
        def _():
            rcopy(RZ.at[i], RZ.at[i], r2_s.at[0], r2_r.at[i], me).wait_recv()

    asum = RZ[0].astype(F32)
    for i in range(1, NZ):
        asum = asum + RZ[i].astype(F32)
    FO[...] = asum[RA:].astype(BF)
    FL[rep, :RA, :] = asum[:RA].astype(BF)

    head, foot = pl.ds(0, RA), pl.ds(RA, RO)

    def home_copy():
        return rcopy(FO, FL.at[zh * 2 + x % 2, foot], t_s.at[0], t_r.at[0], home)

    def home_arrival():
        return rcopy(FO, FL.at[rep, foot], t_s.at[0], t_r.at[0], me)

    def fin(dr, part, ss, rs):
        r = (rep + dr) % NREP
        b = FL.at[rep, part]
        return rcopy(b, b, ss.at[dr - 1], rs.at[rep], (zh, x, c, r // ZL, r % ZL))

    def fin_wait(dr, part, rs):
        r = (rep + dr) % NREP
        b = FL.at[r, part]
        rcopy(b, b, fa_s.at[0], rs.at[r], me).wait_recv()

    @pl.when(hub_other)
    def _():
        home_copy().start()

    @pl.loop(1, NREP)
    def _(dr):
        fin(dr, head, fa_s, fa_r).start()

    @pl.when(hub_self)
    def _():
        FL[rep, RA:, :] = FO[...]

    @pl.when(hub_other)
    def _():
        home_arrival().wait_recv()

    @pl.loop(1, NREP)
    def _(dr):
        fin(dr, foot, fo_s, fo_r).start()

    for s in sends + fwd:
        s.wait_send()

    @pl.when(hub_other)
    def _():
        hub_copy().wait_send()
        home_copy().wait_send()

    @pl.loop(0, NZ)
    def _(i):
        @pl.when(not_self(i))
        def _():
            along_z(WS, WL, w1s, w_r, i).wait_send()
            along_z(OH, OL, o1s, o_r, i).wait_send()

    @pl.loop(0, 24)
    def _(i):
        around_x(WL, w2s, w_r, pix, xr, i).wait_send()
        around_x(OL, o2s, o_r, pix, xr, i).wait_send()

    @pl.loop(0, 8)
    def _(k):
        @pl.when(k_not_self(k))
        def _():
            r2(k).wait_send()

    for i in range(NY):
        dx_sib(i).wait_send()
    for side in range(2):
        dx_far(side).wait_send()
        dx_near(side).wait_send()
        for h in range(2):
            far(h, side).wait_send()
            near(h, side).wait_send()
            summed(h, side).wait_send()

    @pl.loop(1, NREP)
    def _(dr):
        fin_wait(dr, head, fa_r)
        fin_wait(dr, foot, fo_r)
        fin(dr, head, fa_s, fa_r).wait_send()
        fin(dr, foot, fo_s, fo_r).wait_send()

    lane36 = lanes(RP)
    for s in range(3):
        last, lastt = None, None
        for t in range(9):
            if t < 8:
                main = roll(FL[t, RP * s : RP * s + RP, :].astype(F32), 16 * t)
            out = main
            if t > 0:
                prev = jnp.where(lane36 < 16 * (t - 1), last, lastt)
                out = prev if t == 8 else jnp.where(lane36 >= 16 * t, main, prev)
            gw_ref[:, s * D + 128 * t : s * D + 128 * t + 128] = out.astype(gw_ref.dtype)
            if t < 8:
                last = main
                tl = FL[t, 3 * RP : 3 * RP + RP // 2, :].astype(F32)
                halves = [roll(tl, 16 * t - 32 * s - 16 * h) for h in range(2)]
                lastt = jnp.concatenate(halves, axis=0)
    parts = [None] * 3
    for r in range(NREP):
        at = 3 * D + 128 * r
        gw_ref[:, at : at + 128] = FL[r, RA : RA + RP, :].astype(gw_ref.dtype)
        tl = FL[r, RA + RP : RA + RP + 12, :].astype(F32)
        for t in range(3):
            v = roll(jnp.where(lane12 // 16 == t, tl, 0.0), 16 * (r - t))
            parts[t] = v if parts[t] is None else parts[t] + v
    gw_ref[:, 3 * D + 1024 :] = jnp.concatenate(parts, axis=0).astype(gw_ref.dtype)


def vm(*shape, dtype=BF):
    return pltpu.VMEM(shape, dtype)


def local(tokens, out_grad, wq, wk, wv, wo):
    rows = tokens.reshape(-1, D)
    drows = out_grad.reshape(-1, D)
    dma = lambda n: pltpu.SemaphoreType.DMA((n,))
    vmem = pl.BlockSpec(memory_space=pltpu.VMEM)
    hbm = pl.BlockSpec(memory_space=pl.ANY)
    gi, gw = pl.pallas_call(
        kernel,
        out_shape=(
            jax.ShapeDtypeStruct((ROWS, D), BF),
            jax.ShapeDtypeStruct((RP, 4 * D), BF),
        ),
        in_specs=[hbm] * 6,
        out_specs=(vmem, vmem),
        scratch_shapes=[
            vm(NY, 256, D), vm(NY, 256, D), vm(4, RP, D),
            vm(RA, 128), vm(RO, 128), vm(RO, 128), vm(NPIX, RA, 128), vm(NPIX, RO, 128),
            vm(D, 768), vm(256, D), vm(NY, 256, 768), vm(NY, 256, 256),
            vm(NY, 256, D), vm(NY, ROWS, D), vm(3, ROWS, D), vm(2, 64, D), vm(2, ROWS, D),
            vm(D, 768), vm(256, D), vm(NX, 8, RF, 128), vm(8, RF, 128), vm(8, RF, 128),
            vm(8, RF, 128), vm(8, RF, 128), vm(8, RF, 128), vm(NZ, RF, 128),
            vm(RO, 128), vm(NREP, RF, 128),
            dma(6), dma(14), dma(16), dma(1), dma(1), dma(8), dma(24), dma(32),
            dma(8), dma(24), dma(32), dma(4), dma(4), dma(2), dma(2), dma(2), dma(2),
            dma(4), dma(4), dma(4), dma(4), dma(4), dma(4), dma(8), dma(8),
            dma(1), dma(1), dma(7), dma(8), dma(7), dma(8),
        ],
        compiler_params=pltpu.CompilerParams(
            collective_id=0, has_side_effects=True, vmem_limit_bytes=60 * 2**20
        ),
    )(rows, drows, wq, wk, wv, wo)
    return gi.reshape(tokens.shape), gw.astype(F32)


def solution(mesh):
    torus = Mesh(mesh.devices.reshape(ZH, NX, NC, NY, ZL), AXES)
    act = P(AXES, None, None)
    w = P(("zh", "x", "c"), None)
    return jax.shard_map(
        local,
        mesh=torus,
        in_specs=(act, act, w, w, w, w),
        out_specs=(act, w),
        check_vma=False,
    )
```

time: 112 us -> 87 us (0.78)
  Pallas kernels: 107 us -> 83.3 us
  local copies, waits for them, and re-layouts: 3.72 us -> 0.72 us
  other arithmetic: 0 us -> 1.94 us
    pallas_call x1, Pallas kernels: 107 us -> 83.3 us  [local(): pl.pallas_call(kernel, out_shape=(jax.ShapeDtypeStruct((ROWS, D), BF), ja...]
    unnamed x2 -> x3, local copies, waits for them, and re-layouts: 3.72 us -> 0.72 us
    convert_element_type x0 -> x1, other arithmetic: none -> 1.94 us  [local(): return (gi.reshape(tokens.shape), gw.astype(F32))]
where the time goes in v2:
time: 87 us; the launch traced here: 86.6 us
  Pallas kernels  83.3 us (96%)
  other arithmetic  1.94 us (2%)
    pallas_call x1, Pallas kernels, local(): pl.pallas_call(kernel, out_shape=(jax.ShapeDtypeStruct((ROWS, D), BF), ja...  83.3 us
    convert_element_type x1, other arithmetic, local(): return (gi.reshape(tokens.shape), gw.astype(F32))  1.94 us

profile of v2, /device:TPU:1, one launch (start us, length us, event | category | flops | bytes accessed | tf_op | source)
XLA Modules:
  0.0 86.6 jit_solution(548247569444143671)
XLA Ops:
  0.6 83.3 %shard_map.77 = (bf16[128,1152]{1,0:T(8,128)(2,1)}, bf16[36,4608]{1,0:T(8,128)(2,1)}) custom-call(bf16[128,1152]{1,0:T(8,128)(2,1)} %bitcast.4, bf16[128,1152]{1,0:T(8,128)(2,1)} %bitcast.5, bf16[36,1152]{1,0:T(8,128)(2,1)} %wq_ref.1, bf16[36,1152]{1,0:T(8,128)(2,1)} %wk_ref.1, bf16[36,1152]{1,0:T(8,128)(2,1)} %wv_ref.1, bf16[36,1152]{1,0:T(8,128)(2,1)} %wo_ref.1), custom_call_target="tpu_custom_call" | custom-call | tf_op jit(solution)/shard_map/pallas_call | solution.py:618
  84.0 0.0 copy-start
  84.0 1.9 %convert_element_type.3 = f32[36,4608]{1,0:T(8,128)} convert(bf16[36,4608]{1,0:T(8,128)(2,1)} %get-tuple-element.5) | non-fusion elementwise | flops 165888 | bytes 995328 | tf_op jit(solution)/shard_map/convert_element_type | solution.py:643
  85.9 0.0 copy-done
  85.9 0.7 copy.9
Async XLA Ops:
  84.0 2.0 %copy-start = (bf16[128,1152]{1,0:T(8,128)(2,1)S(1)}, bf16[128,1152]{1,0:T(8,128)(2,1)}, u32[]{:S(2)}) copy-start(bf16[128,1152]{1,0:T(8,128)(2,1)} %get-tuple-element.4) | copy-start | bytes 884740

commit v3 on v2

--- a/solution.py
+++ b/solution.py
@@ -48,9 +48,9 @@
 def kernel(
     x_ref, d_ref, wq_ref, wk_ref, wv_ref, wo_ref, gi_ref, gw_ref,
     XA, DA, WIN, WS, OSRC, OH, WL, OL, WCAT, WOC, DQKV, AS, DXP, DXS, DXC, DXH, DXR,
-    DWB, DWOB, DWS, RXA, SMB, RL, RR, R2S, RZ, FO, FL,
+    DWB, DWOB, DWS, RXA, SMB, RL, RR, R2S, RZ, DWO, OXA, OSM, ORL, ORR, O2S, OZ, FO, FL, GI, GW,
     lsem, a_s, a_r, h_s, h_r, w1s, w2s, w_r, o1s, o2s, o_r, xs_s, xs_r, xh_s, xh_r, xy_s, xy_r,
-    a2_s, a2_r, im_s, im_r, sm_s, sm_r, r2_s, r2_r, t_s, t_r, fa_s, fa_r, fo_s, fo_r,
+    a2_s, a2_r, im_s, im_r, sm_s, sm_r, r2_s, r2_r, ro_s, ro_r, t_s, t_r, fa_s, fa_r, fo_s, fo_r,
 ):
     zh, x, c, y, zl = [lax.axis_index(a) for a in AXES]
     pix = (zh * NX + x) * NC + c
@@ -61,10 +61,11 @@
     selfcore = zl == c
     right, left, opp = (y + 1) % NY, (y + 3) % NY, (y + 2) % NY
     xr, xl, xo = (x + 1) % NX, (x + 3) % NX, (x + 2) % NX
-    hub = (y, (x % 2) * 2 + zl, c, zh, x // 2)
-    home = (y, 2 * zl + x // 2, c, zh, x % 2)
-    hub_self = (y == zh) & ((x % 2) * 2 + zl == x) & (zl == x // 2)
-    hub_other = jnp.logical_not(hub_self)
+    pair = jnp.where(x % 2 == 0, (x + 3) % NX, xr)
+    hub = ((2 * zh + 2 - y + 4) % ZH, jnp.where(zl == x // 2, x, pair), c, zh, x // 2)
+    back = jnp.where(x % 2 == 0, (x + 3) % NX, xr)
+    there = x // 2 == zl
+    home = (y, jnp.where(there, x, back), c, (2 * y + 2 - zh + 4) % NY, jnp.where(there, zl, 1 - zl))
 
     def rcopy(src, dst, ss, rs, dev):
         return pltpu.make_async_remote_copy(
@@ -99,10 +100,8 @@
     greet((zh, xr, c, y, zl))
     greet((zh, xl, c, y, zl))
 
-    @pl.when(hub_other)
-    def _():
-        greet(hub)
-        greet(home)
+    greet(hub)
+    greet(home)
 
     ii = lax.broadcasted_iota(jnp.int32, (D, 256), 0)
     nn = lax.broadcasted_iota(jnp.int32, (D, 256), 1)
@@ -127,13 +126,7 @@
     for o in own:
         o.wait()
 
-    @pl.when(hub_self)
-    def _():
-        pl.semaphore_wait(bar, 15 + 6 + 2)
-
-    @pl.when(hub_other)
-    def _():
-        pl.semaphore_wait(bar, 15 + 6 + 2 + 2)
+    pl.semaphore_wait(bar, 15 + 6 + 2 + 2)
 
     def act(kind, yb, cb, to_y, to_c, idx):
         return rcopy(
@@ -150,10 +143,7 @@
         act(0, y, c, y, sib, 4), act(1, y, c, y, sib, 5),
     ]
 
-    @pl.when(hub_other)
-    def _():
-        hub_copy().start()
-
+    hub_copy().start()
     for s in sends[:4]:
         s.start()
 
@@ -171,11 +161,12 @@
         def _():
             buf[pix] = src[...]
 
-        @pl.loop(0, NZ)
-        def _(i):
-            @pl.when(not_self(i))
-            def _():
-                along_z(src, buf, ss, rs, i).start()
+        for dz in (1, 7, 2, 6, 3, 5, 4):
+            along_z(src, buf, ss, rs, (z + dz) % NZ).start()
+
+        @pl.when(jnp.logical_not(selfcore))
+        def _():
+            along_z(src, buf, ss, rs, z).start()
 
     def around_x(buf, ss, rs, p, to, idx):
         return rcopy(buf.at[p], buf.at[p], ss.at[idx], rs.at[p], (zh, to, c, y, zl))
@@ -185,7 +176,9 @@
 
     def both_ways(buf, ss, rs):
         @pl.loop(0, 8)
-        def _(k):
+        def _(n):
+            n = jnp.where(n < 4, n, jnp.where(n < 6, n + 2, n - 2))
+            k = (2 * zh + n) % 8
             p = col(k, x)
 
             @pl.when(jnp.logical_not((p == pix) & selfcore))
@@ -216,17 +209,9 @@
     for s in sends[4:]:
         s.start()
 
-    @pl.when(hub_other)
-    def _():
-        hub_copy().wait_recv()
-
-    @pl.when(hub_self)
-    def _():
-        OH[...] = OSRC[...]
-
+    both_ways(WL, w2s, w_r)
+    hub_copy().wait_recv()
     spread(OH, OL, o1s, o_r)
-    both_ways(WL, w2s, w_r)
-    both_ways(OL, o2s, o_r)
 
     def await_act(kind, yb, cb):
         act(kind, yb, cb, y, sib, 0).wait_recv()
@@ -244,6 +229,7 @@
     fwd[1].start()
     fwd[3].start()
     onward(WL, w2s, w_r)
+    both_ways(OL, o2s, o_r)
     onward(OL, o2s, o_r)
     rest(WL, w_r)
     rest(OL, o_r)
@@ -265,15 +251,22 @@
                     out[at : at + RP // 2, 256 * s + 128 : 256 * s + 256] = v
 
     def oslot(q, r):
-        return ((r // 2) * NX + (q // 2) * 2 + r % 2) * NC + q % 2
+        xs = 2 * c + q // 2
+        other = (xs + 3) % NX if q // 2 == 0 else (xs + 1) % NX
+        xh = jnp.where(c == r % 2, xs, other)
+        return (2 * y + 2 - r // 2 + 4) % ZH, xh, q % 2
+
+    def opix(q, r):
+        zs, xh, cs = oslot(q, r)
+        return (zs * NX + xh) * NC + cs
 
     WOC[COLS:, :] = jnp.zeros((256 - COLS, D), BF)
     lane12 = lanes(12)
     for q in range(4):
         parts = [None] * 3
         for r in range(NREP):
-            WOC[RP * q : RP * q + RP, 128 * r : 128 * r + 128] = OL[oslot(q, r), :RP, :]
-            tl = OL[oslot(q, r), RP : RP + 12, :].astype(F32)
+            WOC[RP * q : RP * q + RP, 128 * r : 128 * r + 128] = OL[opix(q, r), :RP, :]
+            tl = OL[opix(q, r), RP : RP + 12, :].astype(F32)
             for t in range(3):
                 v = jnp.where(lane12 // 16 == t, tl, 0.0)
                 v = roll(v, 16 * (r - t))
@@ -309,7 +302,7 @@
         off = jnp.where(n == 1, 3, jnp.where(n == 2, 1, jnp.where(n == 3, 2, 0)))
         i = (y + off) % NY
 
-        @pl.when(n == 3)
+        @pl.when(n == 2)
         def _():
             await_act(0, opp, c)
             fwd[6].start()
@@ -347,76 +340,112 @@
         DXP[i] = dot_nt(DQKV[i], WCAT[...]).astype(BF)
         dx_sib(i).start()
 
-    dq_all = DQKV[...].reshape(NY * 256, 768)
-
-    @pl.loop(0, 9)
-    def _(i):
-        at = pl.multiple_of(i * 128, 128)
-        lhs = XA[:, :, pl.ds(at, 128)].reshape(NY * 256, 128)
-        DWB[pl.ds(at, 128), :] = dot_tn(lhs, dq_all).astype(BF)
+    OGRP, first_k = 2, (lambda h, side: 4 * side if h == 2 else 2 * h + 4 * side)
+    bufs = lambda h: (DWO, OXA, OSM, ORL, ORR, O2S) if h == OGRP else (DWS, RXA, SMB, RL, RR, R2S)
+
+    def some(h, side):
+        return pl.ds(first_k(h, side), 4 if h == OGRP else 2)
+
+    def to_x(src, dst, ss, rs, h, side):
+        return rcopy(src, dst, ss.at[h * 2 + side], rs.at[h * 2 + side], (zh, (xr, xl)[side], c, y, zl))
+
+    def far(h, side):
+        ks = some(h, side)
+        return to_x(bufs(h)[0].at[xo, ks], bufs(h)[1].at[ks], a2_s, a2_r, h, side)
+
+    def near(h, side):
+        ks = some(h, 1 - side)
+        return to_x(bufs(h)[0].at[(xr, xl)[side], ks], bufs(h)[3 + side].at[ks], im_s, im_r, h, side)
+
+    def summed(h, side):
+        ks = some(h, side)
+        return to_x(bufs(h)[2].at[ks], bufs(h)[3 + side].at[ks], sm_s, sm_r, h, side)
+
+    def start_both(f, h):
+        for side in range(2):
+            f(h, side).start()
+
+    def add_far(h):
+        own_, got, out = bufs(h)[:3]
+        for side in range(2):
+            far(h, side).wait_recv()
+            for k in range(first_k(h, side), first_k(h, side) + (4 if h == OGRP else 2)):
+                out[k] = (own_[(xr, xl)[side], k].astype(F32) + got[k].astype(F32)).astype(BF)
+            summed(h, side).start()
+
+    kown = zh * 2 + c
+
+    def r2(h, k):
+        src, dst, ss, rs = (O2S, OZ, ro_s, ro_r) if h == OGRP else (R2S, RZ, r2_s, r2_r)
+        return rcopy(src.at[k], dst.at[z], ss.at[k], rs.at[z], (k // 2, x, k % 2, y, c))
+
+    def k_not_self(k):
+        return jnp.logical_not((k == kown) & selfcore)
+
+    def send_z(h):
+        for side in range(2):
+            near(h, side).wait_recv()
+            summed(h, side).wait_recv()
+        own_, _, _, fl, fr, out = bufs(h)
+        for side in range(2):
+            for k in range(first_k(h, side), first_k(h, side) + (4 if h == OGRP else 2)):
+                t = own_[x, k].astype(F32) + fl[k].astype(F32) + fr[k].astype(F32)
+                out[k] = t.astype(BF)
+
+                @pl.when(k_not_self(k))
+                def _():
+                    r2(h, k).start()
+
+    def z_sum(h, buf, src):
+        @pl.when(selfcore)
+        def _():
+            buf[z] = src[kown]
+
+        @pl.loop(0, NZ)
+        def _(i):
+            @pl.when(not_self(i))
+            def _():
+                rs = ro_r if h == OGRP else r2_r
+                rcopy(buf.at[i], buf.at[i], r2_s.at[0], rs.at[i], me).wait_recv()
+
+        t = buf[0].astype(F32)
+        for i in range(1, NZ):
+            t = t + buf[i].astype(F32)
+        return t.astype(BF)
 
     DWOB[...] = dot_tn(AS[...].reshape(NY * 256, 256), DA[...].reshape(NY * 256, D)).astype(BF)
-
-    @pl.loop(0, 8)
-    def _(g):
-        src = DWB.at[pl.ds(pl.multiple_of(g * 144, 16), 144)]
-        for q in range(4):
-            p = g * 4 + q
-            x2, k = (p // 2) % NX, (p // 8) * 2 + p % 2
-            base = RP * q
-            tail = None
-            for s in range(3):
-                DWS[x2, k, RP * s : RP * s + RP, :] = src[base : base + RP, 256 * s : 256 * s + 128]
-                t = src[base : base + RP, 256 * s + 128 : 256 * s + 256].astype(F32)
-                t = roll(t[: RP // 2], 32 * s) + roll(t[RP // 2 :], 32 * s + 16)
-                tail = t if tail is None else tail + t
-            DWS[x2, k, 3 * RP : 3 * RP + RP // 2, :] = tail.astype(BF)
-
     for q in range(4):
         tt = [DWOB[RP * q + 12 * t : RP * q + 12 * t + 12, 1024:1152].astype(F32) for t in range(3)]
         for r in range(NREP):
-            p = oslot(q, r)
-            x2, k = (p // 2) % NX, (p // 8) * 2 + p % 2
-            DWS[x2, k, RA : RA + RP, :] = DWOB[RP * q : RP * q + RP, 128 * r : 128 * r + 128]
+            zs, x2, cs = oslot(q, r)
+            k = zs * 2 + cs
+            DWO[x2, k, :RP, :] = DWOB[RP * q : RP * q + RP, 128 * r : 128 * r + 128]
             tail = None
             for t in range(3):
                 v = roll(jnp.where(lane12 // 16 == r, tt[t], 0.0), 16 * (t - r))
                 tail = v if tail is None else tail + v
-            DWS[x2, k, RA + RP : RF, :] = tail.astype(BF)
-
-    def two(k):
-        return pl.ds(k, 2)
-
-    def to_x(src, dst, ss, rs, h, side):
-        return rcopy(src, dst, ss.at[h * 2 + side], rs.at[h * 2 + side], (zh, (xr, xl)[side], c, y, zl))
-
-    def far(h, side):
-        ks = two((2 * h, 4 + 2 * h)[side])
-        return to_x(DWS.at[xo, ks], RXA.at[ks], a2_s, a2_r, h, side)
-
-    def near(h, side):
-        ks = two((4 + 2 * h, 2 * h)[side])
-        return to_x(DWS.at[(xr, xl)[side], ks], (RL, RR)[side].at[ks], im_s, im_r, h, side)
-
-    def summed(h, side):
-        ks = two((2 * h, 4 + 2 * h)[side])
-        return to_x(SMB.at[ks], (RL, RR)[side].at[ks], sm_s, sm_r, h, side)
-
-    def add_far(h):
-        for side in range(2):
-            far(h, side).wait_recv()
-            k0 = (2 * h, 4 + 2 * h)[side]
-            for k in (k0, k0 + 1):
-                t = DWS[(xr, xl)[side], k].astype(F32) + RXA[k].astype(F32)
-                SMB[k] = t.astype(BF)
-            summed(h, side).start()
-
-    for side in range(2):
-        far(0, side).start()
-    for side in range(2):
-        near(0, side).start()
-    for side in range(2):
-        far(1, side).start()
+            DWO[x2, k, RP:RO, :] = tail.astype(BF)
+    start_both(far, OGRP)
+    start_both(near, OGRP)
+
+    dq_all = DQKV[...].reshape(NY * 256, 768)
+
+    def dw_tile(i):
+        lhs = XA[:, :, 128 * i : 128 * i + 128].reshape(NY * 256, 128)
+        DWB[128 * i : 128 * i + 128, :] = dot_tn(lhs, dq_all).astype(BF)
+
+    def pack(g):
+        for q in range(4):
+            p = g * 4 + q
+            x2, k = (p // 2) % NX, (p // 8) * 2 + p % 2
+            base = RP * p
+            tail = None
+            for s in range(3):
+                DWS[x2, k, RP * s : RP * s + RP, :] = DWB[base : base + RP, 256 * s : 256 * s + 128]
+                t = DWB[base : base + RP, 256 * s + 128 : 256 * s + 256].astype(F32)
+                t = roll(t[: RP // 2], 32 * s) + roll(t[RP // 2 :], 32 * s + 16)
+                tail = t if tail is None else tail + t
+            DWS[x2, k, 3 * RP : 3 * RP + RP // 2, :] = tail.astype(BF)
 
     def own_sum(i):
         half = pl.ds(pl.multiple_of(c * ROWS, ROWS), ROWS)
@@ -435,15 +464,26 @@
             (zh, x, c, (right, left)[side], zl),
         )
 
+    for i in (0, 1, 2, 4, 5, 6):
+        dw_tile(i)
+    for g in (0, 1, 4, 5):
+        pack(g)
+    start_both(far, 0)
+    start_both(near, 0)
+    add_far(OGRP)
     for i in range(NY):
         dx_sib(i).wait_recv()
     DXC[0] = own_sum(opp).astype(BF)
     for side in range(2):
         dx_far(side).start()
-
+    for i in (3, 7, 8):
+        dw_tile(i)
+    for g in (2, 3, 6, 7):
+        pack(g)
+    start_both(far, 1)
     add_far(0)
-    for side in range(2):
-        near(1, side).start()
+    start_both(near, 1)
+    send_z(OGRP)
     for side in range(2):
         dx_far(side).wait_recv()
         t = own_sum((right, left)[side])
@@ -456,51 +496,13 @@
         DXC[1 + side, 64:, :] = b.astype(BF)
         dx_near(side).start()
     add_far(1)
-
-    def r2(k):
-        return rcopy(R2S.at[k], RZ.at[z], r2_s.at[k], r2_r.at[z], (k // 2, x, k % 2, y, c))
-
-    kown = zh * 2 + c
-
-    def k_not_self(k):
-        return jnp.logical_not((k == kown) & selfcore)
-
-    for h in range(2):
-        for side in range(2):
-            near(h, side).wait_recv()
-            summed(h, side).wait_recv()
-        for k in (2 * h, 2 * h + 1, 4 + 2 * h, 5 + 2 * h):
-            t = DWS[x, k].astype(F32) + RL[k].astype(F32) + RR[k].astype(F32)
-            R2S[k] = t.astype(BF)
-
-            @pl.when(k_not_self(k))
-            def _():
-                r2(k).start()
-
-    @pl.when(selfcore)
-    def _():
-        RZ[z] = R2S[kown]
-
-    for side in range(2):
-        dx_near(side).wait_recv()
-    gi_ref[...] = (own_sum(y) + DXR[0].astype(F32) + DXR[1].astype(F32)).astype(BF)
-
-    @pl.loop(0, NZ)
-    def _(i):
-        @pl.when(not_self(i))
-        def _():
-            rcopy(RZ.at[i], RZ.at[i], r2_s.at[0], r2_r.at[i], me).wait_recv()
-
-    asum = RZ[0].astype(F32)
-    for i in range(1, NZ):
-        asum = asum + RZ[i].astype(F32)
-    FO[...] = asum[RA:].astype(BF)
-    FL[rep, :RA, :] = asum[:RA].astype(BF)
+    send_z(0)
 
     head, foot = pl.ds(0, RA), pl.ds(RA, RO)
 
     def home_copy():
-        return rcopy(FO, FL.at[zh * 2 + x % 2, foot], t_s.at[0], t_r.at[0], home)
+        r = home[3] * ZL + home[4]
+        return rcopy(FO, FL.at[r, foot], t_s.at[0], t_r.at[0], home)
 
     def home_arrival():
         return rcopy(FO, FL.at[rep, foot], t_s.at[0], t_r.at[0], me)
@@ -515,33 +517,31 @@
         b = FL.at[r, part]
         rcopy(b, b, fa_s.at[0], rs.at[r], me).wait_recv()
 
-    @pl.when(hub_other)
-    def _():
-        home_copy().start()
+    FO[...] = z_sum(OGRP, OZ, O2S)
+    home_copy().start()
+    send_z(1)
+    for side in range(2):
+        dx_near(side).wait_recv()
+    GI[...] = (own_sum(y) + DXR[0].astype(F32) + DXR[1].astype(F32)).astype(BF)
+    gi_out = pltpu.make_async_copy(GI, gi_ref, lsem.at[6])
+    gi_out.start()
+    home_arrival().wait_recv()
+
+    @pl.loop(1, NREP)
+    def _(dr):
+        fin(dr, foot, fo_s, fo_r).start()
+
+    FL[rep, :RA, :] = z_sum(0, RZ, R2S)
 
     @pl.loop(1, NREP)
     def _(dr):
         fin(dr, head, fa_s, fa_r).start()
 
-    @pl.when(hub_self)
-    def _():
-        FL[rep, RA:, :] = FO[...]
-
-    @pl.when(hub_other)
-    def _():
-        home_arrival().wait_recv()
-
-    @pl.loop(1, NREP)
-    def _(dr):
-        fin(dr, foot, fo_s, fo_r).start()
-
     for s in sends + fwd:
         s.wait_send()
 
-    @pl.when(hub_other)
-    def _():
-        hub_copy().wait_send()
-        home_copy().wait_send()
+    hub_copy().wait_send()
+    home_copy().wait_send()
 
     @pl.loop(0, NZ)
     def _(i):
@@ -559,14 +559,15 @@
     def _(k):
         @pl.when(k_not_self(k))
         def _():
-            r2(k).wait_send()
+            r2(0, k).wait_send()
+            r2(OGRP, k).wait_send()
 
     for i in range(NY):
         dx_sib(i).wait_send()
     for side in range(2):
         dx_far(side).wait_send()
         dx_near(side).wait_send()
-        for h in range(2):
+        for h in range(3):
             far(h, side).wait_send()
             near(h, side).wait_send()
             summed(h, side).wait_send()
@@ -588,7 +589,7 @@
             if t > 0:
                 prev = jnp.where(lane36 < 16 * (t - 1), last, lastt)
                 out = prev if t == 8 else jnp.where(lane36 >= 16 * t, main, prev)
-            gw_ref[:, s * D + 128 * t : s * D + 128 * t + 128] = out.astype(gw_ref.dtype)
+            GW[:, s * D + 128 * t : s * D + 128 * t + 128] = out.astype(GW.dtype)
             if t < 8:
                 last = main
                 tl = FL[t, 3 * RP : 3 * RP + RP // 2, :].astype(F32)
@@ -597,12 +598,16 @@
     parts = [None] * 3
     for r in range(NREP):
         at = 3 * D + 128 * r
-        gw_ref[:, at : at + 128] = FL[r, RA : RA + RP, :].astype(gw_ref.dtype)
+        GW[:, at : at + 128] = FL[r, RA : RA + RP, :].astype(GW.dtype)
         tl = FL[r, RA + RP : RA + RP + 12, :].astype(F32)
         for t in range(3):
             v = roll(jnp.where(lane12 // 16 == t, tl, 0.0), 16 * (r - t))
             parts[t] = v if parts[t] is None else parts[t] + v
-    gw_ref[:, 3 * D + 1024 :] = jnp.concatenate(parts, axis=0).astype(gw_ref.dtype)
+    GW[:, 3 * D + 1024 :] = jnp.concatenate(parts, axis=0).astype(GW.dtype)
+    gw_out = pltpu.make_async_copy(GW, gw_ref, lsem.at[7])
+    gw_out.start()
+    gi_out.wait()
+    gw_out.wait()
 
 
 def vm(*shape, dtype=BF):
@@ -613,7 +618,6 @@
     rows = tokens.reshape(-1, D)
     drows = out_grad.reshape(-1, D)
     dma = lambda n: pltpu.SemaphoreType.DMA((n,))
-    vmem = pl.BlockSpec(memory_space=pltpu.VMEM)
     hbm = pl.BlockSpec(memory_space=pl.ANY)
     gi, gw = pl.pallas_call(
         kernel,
@@ -622,18 +626,18 @@
             jax.ShapeDtypeStruct((RP, 4 * D), BF),
         ),
         in_specs=[hbm] * 6,
-        out_specs=(vmem, vmem),
+        out_specs=(hbm, hbm),
         scratch_shapes=[
             vm(NY, 256, D), vm(NY, 256, D), vm(4, RP, D),
             vm(RA, 128), vm(RO, 128), vm(RO, 128), vm(NPIX, RA, 128), vm(NPIX, RO, 128),
             vm(D, 768), vm(256, D), vm(NY, 256, 768), vm(NY, 256, 256),
             vm(NY, 256, D), vm(NY, ROWS, D), vm(3, ROWS, D), vm(2, 64, D), vm(2, ROWS, D),
-            vm(D, 768), vm(256, D), vm(NX, 8, RF, 128), vm(8, RF, 128), vm(8, RF, 128),
-            vm(8, RF, 128), vm(8, RF, 128), vm(8, RF, 128), vm(NZ, RF, 128),
-            vm(RO, 128), vm(NREP, RF, 128),
-            dma(6), dma(14), dma(16), dma(1), dma(1), dma(8), dma(24), dma(32),
+            vm(D, 768), vm(256, D), vm(NX, 8, RA, 128), *[vm(8, RA, 128)] * 5, vm(NZ, RA, 128),
+            vm(NX, 8, RO, 128), *[vm(8, RO, 128)] * 5, vm(NZ, RO, 128),
+            vm(RO, 128), vm(NREP, RF, 128), vm(ROWS, D), vm(RP, 4 * D),
+            dma(8), dma(14), dma(16), dma(1), dma(1), dma(8), dma(24), dma(32),
             dma(8), dma(24), dma(32), dma(4), dma(4), dma(2), dma(2), dma(2), dma(2),
-            dma(4), dma(4), dma(4), dma(4), dma(4), dma(4), dma(8), dma(8),
+            dma(6), dma(6), dma(6), dma(6), dma(6), dma(6), dma(8), dma(8), dma(8), dma(8),
             dma(1), dma(1), dma(7), dma(8), dma(7), dma(8),
         ],
         compiler_params=pltpu.CompilerParams(

time: 87 us -> 77.3 us (0.89)
  Pallas kernels: 83.3 us -> 73.8 us
    pallas_call x1, Pallas kernels: 83.3 us -> 73.8 us  [local(): pl.pallas_call(kernel, out_shape=(jax.ShapeDtypeStruct((ROWS, D), BF), ja...]
where the time goes in v3:
time: 77.3 us; the launch traced here: 77.1 us
  Pallas kernels  73.8 us (95%)
  other arithmetic  1.94 us (3%)
    pallas_call x1, Pallas kernels, local(): pl.pallas_call(kernel, out_shape=(jax.ShapeDtypeStruct((ROWS, D), BF), ja...  73.8 us
    convert_element_type x1, other arithmetic, local(): return (gi.reshape(tokens.shape), gw.astype(F32))  1.94 us

profile of v3, /device:TPU:1, one launch (start us, length us, event | category | flops | bytes accessed | tf_op | source)
XLA Modules:
  0.0 77.1 jit_solution(1149759283026170838)
XLA Ops:
  0.6 73.8 %shard_map.77 = (bf16[128,1152]{1,0:T(8,128)(2,1)}, bf16[36,4608]{1,0:T(8,128)(2,1)}) custom-call(bf16[128,1152]{1,0:T(8,128)(2,1)} %bitcast.4, bf16[128,1152]{1,0:T(8,128)(2,1)} %bitcast.5, bf16[36,1152]{1,0:T(8,128)(2,1)} %wq_ref.1, bf16[36,1152]{1,0:T(8,128)(2,1)} %wk_ref.1, bf16[36,1152]{1,0:T(8,128)(2,1)} %wv_ref.1, bf16[36,1152]{1,0:T(8,128)(2,1)} %wo_ref.1), custom_call_target="tpu_custom_call" | custom-call | tf_op jit(solution)/shard_map/pallas_call | solution.py:622
  74.4 0.0 copy-start
  74.4 1.9 %convert_element_type.3 = f32[36,4608]{1,0:T(8,128)} convert(bf16[36,4608]{1,0:T(8,128)(2,1)} %get-tuple-element.5) | non-fusion elementwise | flops 165888 | bytes 995328 | tf_op jit(solution)/shard_map/convert_element_type | solution.py:647
  76.3 0.0 copy-done
  76.4 0.7 copy.9
Async XLA Ops:
  74.4 2.0 %copy-start = (bf16[128,1152]{1,0:T(8,128)(2,1)S(1)}, bf16[128,1152]{1,0:T(8,128)(2,1)}, u32[]{:S(2)}) copy-start(bf16[128,1152]{1,0:T(8,128)(2,1)} %get-tuple-element.4) | copy-start | bytes 884740

commit v4 on v3

--- a/solution.py
+++ b/solution.py
@@ -49,8 +49,7 @@
     x_ref, d_ref, wq_ref, wk_ref, wv_ref, wo_ref, gi_ref, gw_ref,
     XA, DA, WIN, WS, OSRC, OH, WL, OL, WCAT, WOC, DQKV, AS, DXP, DXS, DXC, DXH, DXR,
     DWB, DWOB, DWS, RXA, SMB, RL, RR, R2S, RZ, DWO, OXA, OSM, ORL, ORR, O2S, OZ, FO, FL, GI, GW,
-    lsem, a_s, a_r, h_s, h_r, w1s, w2s, w_r, o1s, o2s, o_r, xs_s, xs_r, xh_s, xh_r, xy_s, xy_r,
-    a2_s, a2_r, im_s, im_r, sm_s, sm_r, r2_s, r2_r, ro_s, ro_r, t_s, t_r, fa_s, fa_r, fo_s, fo_r,
+    lsem, sent, a_r, s_r, h_r, w_r, o_r, dx_r, xh_r, far_r, near_r, z_r, t_r, f_r,
 ):
     zh, x, c, y, zl = [lax.axis_index(a) for a in AXES]
     pix = (zh * NX + x) * NC + c
@@ -129,13 +128,11 @@
     pl.semaphore_wait(bar, 15 + 6 + 2 + 2)
 
     def act(kind, yb, cb, to_y, to_c, idx):
-        return rcopy(
-            blk(kind, yb, cb), blk(kind, yb, cb), a_s.at[idx],
-            a_r.at[kind * 8 + yb * 2 + cb], (zh, x, to_c, to_y, zl),
-        )
+        rs = s_r.at[yb] if to_c is sib else a_r.at[kind * 4 + yb]
+        return rcopy(blk(kind, yb, cb), blk(kind, yb, cb), sent.at[idx // 6], rs, (zh, x, to_c, to_y, zl))
 
     def hub_copy():
-        return rcopy(OSRC, OH, h_s.at[0], h_r.at[0], hub)
+        return rcopy(OSRC, OH, sent.at[3], h_r.at[0], hub)
 
     sends = [
         act(0, y, c, right, c, 0), act(1, y, c, left, c, 1),
@@ -151,7 +148,7 @@
         return ((k // 2) * NX + xs) * NC + k % 2
 
     def along_z(src, buf, ss, rs, i):
-        return rcopy(src, buf.at[pix], ss.at[i], rs.at[pix], (i // 2, x, zl, y, i % 2))
+        return rcopy(src, buf.at[pix], sent.at[ss], rs.at[zh * 2 + c], (i // 2, x, zl, y, i % 2))
 
     def not_self(i):
         return jnp.logical_not((i == z) & selfcore)
@@ -169,13 +166,13 @@
             along_z(src, buf, ss, rs, z).start()
 
     def around_x(buf, ss, rs, p, to, idx):
-        return rcopy(buf.at[p], buf.at[p], ss.at[idx], rs.at[p], (zh, to, c, y, zl))
-
-    def arrived(buf, rs, p):
-        rcopy(buf.at[p], buf.at[p], w1s.at[0], rs.at[p], me).wait_recv()
-
-    def both_ways(buf, ss, rs):
-        @pl.loop(0, 8)
+        return rcopy(buf.at[p], buf.at[p], sent.at[ss + 1], rs.at[idx], (zh, to, c, y, zl))
+
+    def arrived(ref, rs, idx):
+        rcopy(ref, ref, sent.at[0], rs.at[idx], me).wait_recv()
+
+    def both_ways(buf, ss, rs, lo, hi):
+        @pl.loop(lo, hi)
         def _(n):
             n = jnp.where(n < 4, n, jnp.where(n < 6, n + 2, n - 2))
             k = (2 * zh + n) % 8
@@ -183,38 +180,39 @@
 
             @pl.when(jnp.logical_not((p == pix) & selfcore))
             def _():
-                arrived(buf, rs, p)
-
-            around_x(buf, ss, rs, p, xr, k).start()
-            around_x(buf, ss, rs, p, xl, 8 + k).start()
-
-    def onward(buf, ss, rs):
-        @pl.loop(0, 4)
-        def _(k):
-            p, q = col(k, xl), col(k + 4, xr)
-            arrived(buf, rs, p)
-            around_x(buf, ss, rs, p, xr, 16 + k).start()
-            arrived(buf, rs, q)
-            around_x(buf, ss, rs, q, xl, 20 + k).start()
+                arrived(buf.at[p], rs, k)
+
+            around_x(buf, ss, rs, p, xr, jnp.where(k % 2 == 0, 8 + k, 16)).start()
+            around_x(buf, ss, rs, p, xl, jnp.where(k % 2 == 0, 16, 8 + k)).start()
+
+    def onward(buf, ss, rs, lo, hi):
+        @pl.loop(lo, hi)
+        def _(n):
+            k = 2 * ((zh + jnp.where(n < 2, n, 5 - n)) % ZH)
+            p, q = col(k, xl), col(k + 1, xr)
+            arrived(buf.at[p], rs, 8 + k)
+            around_x(buf, ss, rs, p, xr, 16).start()
+            arrived(buf.at[q], rs, 9 + k)
+            around_x(buf, ss, rs, q, xl, 16).start()
 
     def rest(buf, rs):
-        @pl.loop(0, 4)
-        def _(k):
-            arrived(buf, rs, col(k + 4, xl))
-            arrived(buf, rs, col(k, xr))
-            arrived(buf, rs, col(k, xo))
-            arrived(buf, rs, col(k + 4, xo))
-
-    spread(WS, WL, w1s, w_r)
+        arrived(buf.at[pl.ds(0, 16)], rs, 16)
+
+    spread(WS, WL, 4, w_r)
     for s in sends[4:]:
         s.start()
-
-    both_ways(WL, w2s, w_r)
+    both_ways(WL, 4, w_r, 0, 2)
     hub_copy().wait_recv()
-    spread(OH, OL, o1s, o_r)
-
-    def await_act(kind, yb, cb):
-        act(kind, yb, cb, y, sib, 0).wait_recv()
+    spread(OH, OL, 6, o_r)
+    both_ways(WL, 4, w_r, 2, 4)
+    onward(WL, 4, w_r, 0, 2)
+    both_ways(WL, 4, w_r, 4, 8)
+
+    def await_act(kind, yb):
+        rcopy(blk(kind, yb, c), blk(kind, yb, c), sent.at[0], a_r.at[kind * 4 + yb], me).wait_recv()
+
+    def await_sib(yb):
+        rcopy(XA.at[yb], XA.at[yb], sent.at[0], s_r.at[yb], me).wait_recv()
 
     fwd = [
         act(0, left, c, right, c, 6), act(1, right, c, left, c, 7),
@@ -222,17 +220,16 @@
         act(1, left, c, y, sib, 10), act(0, right, c, y, sib, 11),
         act(0, opp, c, y, sib, 12), act(1, opp, c, y, sib, 13),
     ]
-    await_act(0, left, c)
+    await_act(0, left)
     fwd[0].start()
     fwd[2].start()
-    await_act(1, right, c)
+    await_act(1, right)
     fwd[1].start()
     fwd[3].start()
-    onward(WL, w2s, w_r)
-    both_ways(OL, o2s, o_r)
-    onward(OL, o2s, o_r)
+    both_ways(OL, 6, o_r, 0, 8)
+    onward(WL, 4, w_r, 2, 4)
+    onward(OL, 6, o_r, 0, 4)
     rest(WL, w_r)
-    rest(OL, o_r)
 
     low16 = lanes(RP // 2) < 16
 
@@ -249,6 +246,54 @@
                     v = jnp.where(low16, roll(tl, -(32 * s + 16 * half)), 0.0).astype(BF)
                     at = base + half * (RP // 2)
                     out[at : at + RP // 2, 256 * s + 128 : 256 * s + 256] = v
+
+    scale = 1.0 / HEAD_DIM**0.5
+    row = lax.broadcasted_iota(jnp.int32, (ROWS, 128), 0)
+    col_ = lax.broadcasted_iota(jnp.int32, (ROWS, 128), 1)
+    inside = row // FRAMES == col_ // FRAMES
+    lane256 = lax.broadcasted_iota(jnp.int32, (ROWS, 256), 1)
+    first = lane256 < HEAD_DIM
+    zero = jnp.zeros((ROWS, 256), BF)
+
+    def two_heads(v):
+        return jnp.concatenate([jnp.where(first, v, zero), jnp.where(first, zero, v)], axis=0)
+
+    def chunk(ids):
+        qkv = dot_nn(jnp.concatenate([XA[i] for i in ids], axis=0), WCAT[...]).astype(BF)
+        da = dot_nt(jnp.concatenate([DA[i] for i in ids], axis=0), WOC[...]).astype(BF)
+        for h in range(2 * len(ids)):
+            i, rs, at = ids[h // 2], pl.ds(h % 2 * ROWS, ROWS), slice(h * ROWS, h * ROWS + ROWS)
+            q, k, v, g = qkv[at, :256], qkv[at, 256:512], qkv[at, 512:], da[at]
+            kk, vv = two_heads(k), two_heads(v)
+            sc = dot_nt(kk, q) * scale
+            dp = dot_nt(vv, g)
+            probs, dscore = [], []
+            for n2 in range(2):
+                cs = slice(n2 * 128, n2 * 128 + 128)
+                s1 = jnp.where(inside, sc[cs], -jnp.inf)
+                e = jnp.exp(s1 - jnp.max(s1, axis=0, keepdims=True))
+                p1 = e * (1.0 / jnp.sum(e, axis=0, keepdims=True))
+                d1 = dp[cs]
+                t1 = jnp.sum(d1 * p1, axis=0, keepdims=True)
+                probs.append(p1.astype(BF))
+                dscore.append((p1 * (d1 - t1) * scale).astype(BF))
+            pb = jnp.concatenate(probs, axis=0)
+            ds = jnp.concatenate(dscore, axis=0)
+            AS[i, rs, :] = dot_tn(pb, vv).astype(BF)
+            DQKV[i, rs, :256] = dot_tn(ds, kk).astype(BF)
+            dk = dot_nn(ds, q)
+            DQKV[i, rs, 256:512] = jnp.where(first, dk[:128], dk[128:]).astype(BF)
+            dv = dot_nn(pb, g)
+            DQKV[i, rs, 512:] = jnp.where(first, dv[:128], dv[128:]).astype(BF)
+        back = dot_nt(jnp.concatenate([DQKV[i] for i in ids], axis=0), WCAT[...]).astype(BF)
+        for m, i in enumerate(ids):
+            DXP[i] = back[256 * m : 256 * m + 256]
+
+    await_act(1, left)
+    fwd[4].start()
+    await_act(0, right)
+    fwd[5].start()
+    rest(OL, o_r)
 
     def oslot(q, r):
         xs = 2 * c + q // 2
@@ -275,26 +320,10 @@
             at = RP * q + 12 * t
             WOC[at : at + 12, 1024:1152] = parts[t].astype(BF)
 
-    await_act(1, left, c)
-    fwd[4].start()
-    await_act(0, right, c)
-    fwd[5].start()
-
-    scale = 1.0 / HEAD_DIM**0.5
-    row = lax.broadcasted_iota(jnp.int32, (ROWS, 128), 0)
-    col_ = lax.broadcasted_iota(jnp.int32, (ROWS, 128), 1)
-    inside = row // FRAMES == col_ // FRAMES
-    lane256 = lax.broadcasted_iota(jnp.int32, (ROWS, 256), 1)
-    first = lane256 < HEAD_DIM
-    zero = jnp.zeros((ROWS, 256), BF)
-
-    def two_heads(v):
-        return jnp.concatenate([jnp.where(first, v, zero), jnp.where(first, zero, v)], axis=0)
-
     def dx_sib(i):
         return rcopy(
             DXP.at[i, pl.ds(pl.multiple_of(sib * ROWS, ROWS), ROWS)], DXS.at[i],
-            xs_s.at[i], xs_r.at[i], (zh, x, sib, y, zl),
+            sent.at[8], dx_r.at[0], (zh, x, sib, y, zl),
         )
 
     @pl.loop(0, NY)
@@ -304,62 +333,35 @@
 
         @pl.when(n == 2)
         def _():
-            await_act(0, opp, c)
+            await_act(0, opp)
             fwd[6].start()
-            await_act(1, opp, c)
+            await_act(1, opp)
             fwd[7].start()
 
-        await_act(0, i, sib)
-        await_act(1, i, sib)
-        qkv = dot_nn(XA[i], WCAT[...]).astype(BF)
-        da = dot_nt(DA[i], WOC[...]).astype(BF)
-        for h in range(2):
-            rs = slice(h * ROWS, h * ROWS + ROWS)
-            q, k, v, g = qkv[rs, :256], qkv[rs, 256:512], qkv[rs, 512:], da[rs]
-            kk, vv = two_heads(k), two_heads(v)
-            sc = dot_nt(q, kk) * scale
-            dp = dot_nt(g, vv)
-            probs, dscore = [], []
-            for n2 in range(2):
-                cs = slice(n2 * 128, n2 * 128 + 128)
-                s1 = jnp.where(inside, sc[:, cs], -jnp.inf)
-                e = jnp.exp(s1 - jnp.max(s1, axis=1, keepdims=True))
-                p1 = e / jnp.sum(e, axis=1, keepdims=True)
-                d1 = dp[:, cs]
-                t1 = jnp.sum(d1 * p1, axis=1, keepdims=True)
-                probs.append(p1.astype(BF))
-                dscore.append((p1 * (d1 - t1) * scale).astype(BF))
-            pb = jnp.concatenate(probs, axis=1)
-            ds = jnp.concatenate(dscore, axis=1)
-            AS[i, rs, :] = dot_nn(pb, vv).astype(BF)
-            DQKV[i, rs, :256] = dot_nn(ds, kk).astype(BF)
-            dk = dot_tn(ds, q)
-            DQKV[i, rs, 256:512] = jnp.where(first, dk[:128], dk[128:]).astype(BF)
-            dv = dot_tn(pb, g)
-            DQKV[i, rs, 512:] = jnp.where(first, dv[:128], dv[128:]).astype(BF)
-        DXP[i] = dot_nt(DQKV[i], WCAT[...]).astype(BF)
+        await_sib(i)
+        chunk((i,))
         dx_sib(i).start()
 
-    OGRP, first_k = 2, (lambda h, side: 4 * side if h == 2 else 2 * h + 4 * side)
+    OGRP, first_k = 4, (lambda h, side: 4 * side + h % 4)
     bufs = lambda h: (DWO, OXA, OSM, ORL, ORR, O2S) if h == OGRP else (DWS, RXA, SMB, RL, RR, R2S)
 
     def some(h, side):
-        return pl.ds(first_k(h, side), 4 if h == OGRP else 2)
-
-    def to_x(src, dst, ss, rs, h, side):
-        return rcopy(src, dst, ss.at[h * 2 + side], rs.at[h * 2 + side], (zh, (xr, xl)[side], c, y, zl))
+        return pl.ds(first_k(h, side), 4 if h == OGRP else 1)
+
+    def to_x(src, dst, rs, h, side):
+        return rcopy(src, dst, sent.at[9 + (h == OGRP)], rs, (zh, (xr, xl)[side], c, y, zl))
 
     def far(h, side):
         ks = some(h, side)
-        return to_x(bufs(h)[0].at[xo, ks], bufs(h)[1].at[ks], a2_s, a2_r, h, side)
+        return to_x(bufs(h)[0].at[xo, ks], bufs(h)[1].at[ks], far_r.at[h * 2 + side], h, side)
 
     def near(h, side):
         ks = some(h, 1 - side)
-        return to_x(bufs(h)[0].at[(xr, xl)[side], ks], bufs(h)[3 + side].at[ks], im_s, im_r, h, side)
+        return to_x(bufs(h)[0].at[(xr, xl)[side], ks], bufs(h)[3 + side].at[ks], near_r.at[h], h, side)
 
     def summed(h, side):
         ks = some(h, side)
-        return to_x(bufs(h)[2].at[ks], bufs(h)[3 + side].at[ks], sm_s, sm_r, h, side)
+        return to_x(bufs(h)[2].at[ks], bufs(h)[3 + side].at[ks], near_r.at[h], h, side)
 
     def start_both(f, h):
         for side in range(2):
@@ -369,26 +371,24 @@
         own_, got, out = bufs(h)[:3]
         for side in range(2):
             far(h, side).wait_recv()
-            for k in range(first_k(h, side), first_k(h, side) + (4 if h == OGRP else 2)):
+            for k in range(first_k(h, side), first_k(h, side) + (4 if h == OGRP else 1)):
                 out[k] = (own_[(xr, xl)[side], k].astype(F32) + got[k].astype(F32)).astype(BF)
             summed(h, side).start()
 
     kown = zh * 2 + c
 
     def r2(h, k):
-        src, dst, ss, rs = (O2S, OZ, ro_s, ro_r) if h == OGRP else (R2S, RZ, r2_s, r2_r)
-        return rcopy(src.at[k], dst.at[z], ss.at[k], rs.at[z], (k // 2, x, k % 2, y, c))
+        src, dst, o = (O2S, OZ, 1) if h == OGRP else (R2S, RZ, 0)
+        return rcopy(src.at[k], dst.at[z], sent.at[11 + o], z_r.at[o], (k // 2, x, k % 2, y, c))
 
     def k_not_self(k):
         return jnp.logical_not((k == kown) & selfcore)
 
     def send_z(h):
-        for side in range(2):
-            near(h, side).wait_recv()
-            summed(h, side).wait_recv()
+        arrived(DWO.at[pl.ds(0, 2)] if h == OGRP else RL.at[pl.ds(0, 4)], near_r, h)
         own_, _, _, fl, fr, out = bufs(h)
         for side in range(2):
-            for k in range(first_k(h, side), first_k(h, side) + (4 if h == OGRP else 2)):
+            for k in range(first_k(h, side), first_k(h, side) + (4 if h == OGRP else 1)):
                 t = own_[x, k].astype(F32) + fl[k].astype(F32) + fr[k].astype(F32)
                 out[k] = t.astype(BF)
 
@@ -401,12 +401,13 @@
         def _():
             buf[z] = src[kown]
 
-        @pl.loop(0, NZ)
-        def _(i):
-            @pl.when(not_self(i))
-            def _():
-                rs = ro_r if h == OGRP else r2_r
-                rcopy(buf.at[i], buf.at[i], r2_s.at[0], rs.at[i], me).wait_recv()
+        @pl.when(selfcore)
+        def _():
+            arrived(buf.at[pl.ds(0, 7)], z_r, h // 4)
+
+        @pl.when(jnp.logical_not(selfcore))
+        def _():
+            arrived(buf, z_r, h // 4)
 
         t = buf[0].astype(F32)
         for i in range(1, NZ):
@@ -454,13 +455,13 @@
     def dx_far(side):
         rows = pl.ds(64 * side, 64)
         return rcopy(
-            DXC.at[0, rows], DXH.at[side], xh_s.at[side], xh_r.at[side],
+            DXC.at[0, rows], DXH.at[side], sent.at[13], xh_r.at[side],
             (zh, x, c, (right, left)[side], zl),
         )
 
     def dx_near(side):
         return rcopy(
-            DXC.at[1 + side], DXR.at[side], xy_s.at[side], xy_r.at[side],
+            DXC.at[1 + side], DXR.at[side], sent.at[14], dx_r.at[1],
             (zh, x, c, (right, left)[side], zl),
         )
 
@@ -470,9 +471,9 @@
         pack(g)
     start_both(far, 0)
     start_both(near, 0)
+    start_both(far, 1)
     add_far(OGRP)
-    for i in range(NY):
-        dx_sib(i).wait_recv()
+    arrived(DXS, dx_r, 0)
     DXC[0] = own_sum(opp).astype(BF)
     for side in range(2):
         dx_far(side).start()
@@ -480,9 +481,12 @@
         dw_tile(i)
     for g in (2, 3, 6, 7):
         pack(g)
-    start_both(far, 1)
+    start_both(far, 2)
     add_far(0)
     start_both(near, 1)
+    add_far(1)
+    start_both(far, 3)
+    start_both(near, 2)
     send_z(OGRP)
     for side in range(2):
         dx_far(side).wait_recv()
@@ -495,89 +499,78 @@
         DXC[1 + side, :64, :] = a.astype(BF)
         DXC[1 + side, 64:, :] = b.astype(BF)
         dx_near(side).start()
-    add_far(1)
+    add_far(2)
+    start_both(near, 3)
     send_z(0)
+    add_far(3)
+    send_z(1)
 
     head, foot = pl.ds(0, RA), pl.ds(RA, RO)
 
     def home_copy():
         r = home[3] * ZL + home[4]
-        return rcopy(FO, FL.at[r, foot], t_s.at[0], t_r.at[0], home)
+        return rcopy(FO, FL.at[r, foot], sent.at[15], t_r.at[0], home)
 
     def home_arrival():
-        return rcopy(FO, FL.at[rep, foot], t_s.at[0], t_r.at[0], me)
-
-    def fin(dr, part, ss, rs):
+        return rcopy(FO, FL.at[rep, foot], sent.at[15], t_r.at[0], me)
+
+    def fin(dr, part, o):
         r = (rep + dr) % NREP
         b = FL.at[rep, part]
-        return rcopy(b, b, ss.at[dr - 1], rs.at[rep], (zh, x, c, r // ZL, r % ZL))
-
-    def fin_wait(dr, part, rs):
-        r = (rep + dr) % NREP
-        b = FL.at[r, part]
-        rcopy(b, b, fa_s.at[0], rs.at[r], me).wait_recv()
+        return rcopy(b, b, sent.at[16 + o], f_r.at[o], (zh, x, c, r // ZL, r % ZL))
 
     FO[...] = z_sum(OGRP, OZ, O2S)
     home_copy().start()
-    send_z(1)
-    for side in range(2):
-        dx_near(side).wait_recv()
+    send_z(2)
+    send_z(3)
+    home_arrival().wait_recv()
+
+    @pl.loop(1, NREP)
+    def _(dr):
+        fin(dr, foot, 1).start()
+
+    FL[rep, :RA, :] = z_sum(0, RZ, R2S)
+
+    @pl.loop(1, NREP)
+    def _(dr):
+        fin(dr, head, 0).start()
+
+    arrived(DXR, dx_r, 1)
     GI[...] = (own_sum(y) + DXR[0].astype(F32) + DXR[1].astype(F32)).astype(BF)
     gi_out = pltpu.make_async_copy(GI, gi_ref, lsem.at[6])
     gi_out.start()
-    home_arrival().wait_recv()
-
-    @pl.loop(1, NREP)
-    def _(dr):
-        fin(dr, foot, fo_s, fo_r).start()
-
-    FL[rep, :RA, :] = z_sum(0, RZ, R2S)
-
-    @pl.loop(1, NREP)
-    def _(dr):
-        fin(dr, head, fa_s, fa_r).start()
-
-    for s in sends + fwd:
-        s.wait_send()
-
+
+    def left_from(ref, idx):
+        rcopy(ref, ref, sent.at[idx], t_r.at[0], me).wait_send()
+
+    left_from(XA.at[pl.ds(0, 3)], 0)
+    left_from(XA.at[pl.ds(0, 3)], 1)
+    left_from(XA.at[0], 2)
     hub_copy().wait_send()
+
+    @pl.when(selfcore)
+    def _():
+        for b, idx in ((WL, 4), (OL, 6), (RZ, 11), (OZ, 12)):
+            left_from(b.at[pl.ds(0, 7)], idx)
+
+    @pl.when(jnp.logical_not(selfcore))
+    def _():
+        for b, idx in ((WL, 4), (OL, 6), (RZ, 11), (OZ, 12)):
+            left_from(b.at[pl.ds(0, 8)], idx)
+
+    left_from(WL.at[pl.ds(0, 24)], 5)
+    left_from(OL.at[pl.ds(0, 24)], 7)
+    left_from(DXS, 8)
+    left_from(DWS.at[pl.ds(0, 3)], 9)
+    left_from(DWO.at[pl.ds(0, 3)], 10)
+    left_from(DXH, 13)
+    left_from(DXR, 14)
     home_copy().wait_send()
 
-    @pl.loop(0, NZ)
-    def _(i):
-        @pl.when(not_self(i))
-        def _():
-            along_z(WS, WL, w1s, w_r, i).wait_send()
-            along_z(OH, OL, o1s, o_r, i).wait_send()
-
-    @pl.loop(0, 24)
-    def _(i):
-        around_x(WL, w2s, w_r, pix, xr, i).wait_send()
-        around_x(OL, o2s, o_r, pix, xr, i).wait_send()
-
-    @pl.loop(0, 8)
-    def _(k):
-        @pl.when(k_not_self(k))
-        def _():
-            r2(0, k).wait_send()
-            r2(OGRP, k).wait_send()
-
-    for i in range(NY):
-        dx_sib(i).wait_send()
-    for side in range(2):
-        dx_far(side).wait_send()
-        dx_near(side).wait_send()
-        for h in range(3):
-            far(h, side).wait_send()
-            near(h, side).wait_send()
-            summed(h, side).wait_send()
-
-    @pl.loop(1, NREP)
-    def _(dr):
-        fin_wait(dr, head, fa_r)
-        fin_wait(dr, foot, fo_r)
-        fin(dr, head, fa_s, fa_r).wait_send()
-        fin(dr, foot, fo_s, fo_r).wait_send()
+    for o, part in enumerate((head, foot)):
+        b = FL.at[pl.ds(0, 7), part]
+        arrived(b, f_r, o)
+        left_from(b, 16 + o)
 
     lane36 = lanes(RP)
     for s in range(3):
@@ -635,10 +628,8 @@
             vm(D, 768), vm(256, D), vm(NX, 8, RA, 128), *[vm(8, RA, 128)] * 5, vm(NZ, RA, 128),
             vm(NX, 8, RO, 128), *[vm(8, RO, 128)] * 5, vm(NZ, RO, 128),
             vm(RO, 128), vm(NREP, RF, 128), vm(ROWS, D), vm(RP, 4 * D),
-            dma(8), dma(14), dma(16), dma(1), dma(1), dma(8), dma(24), dma(32),
-            dma(8), dma(24), dma(32), dma(4), dma(4), dma(2), dma(2), dma(2), dma(2),
-            dma(6), dma(6), dma(6), dma(6), dma(6), dma(6), dma(8), dma(8), dma(8), dma(8),
-            dma(1), dma(1), dma(7), dma(8), dma(7), dma(8),
+            dma(8), dma(20), dma(8), dma(4), dma(1), dma(17), dma(17), dma(2), dma(2), dma(10),
+            dma(5), dma(2), dma(1), dma(4),
         ],
         compiler_params=pltpu.CompilerParams(
             collective_id=0, has_side_effects=True, vmem_limit_bytes=60 * 2**20

time: 77.3 us -> 72.9 us (0.943); the launches traced: 77.1 us -> 71.9 us
  Pallas kernels: 73.8 us -> 68.6 us
    pallas_call x1, Pallas kernels: 73.8 us -> 68.6 us  [local(): pl.pallas_call(kernel, out_shape=(jax.ShapeDtypeStruct((ROWS, D), BF), ja...]
where the time goes in v4:
time: 72.9 us; the launch traced here: 71.9 us
  Pallas kernels  68.6 us (94%)
  other arithmetic  1.94 us (3%)
    pallas_call x1, Pallas kernels, local(): pl.pallas_call(kernel, out_shape=(jax.ShapeDtypeStruct((ROWS, D), BF), ja...  68.6 us
    convert_element_type x1, other arithmetic, local(): return (gi.reshape(tokens.shape), gw.astype(F32))  1.94 us

profile of v4, /device:TPU:1, one launch (start us, length us, event | category | flops | bytes accessed | tf_op | source)
XLA Modules:
  0.0 71.9 jit_solution(9393545012227654158)
XLA Ops:
  0.6 68.6 %shard_map.77 = (bf16[128,1152]{1,0:T(8,128)(2,1)}, bf16[36,4608]{1,0:T(8,128)(2,1)}) custom-call(bf16[128,1152]{1,0:T(8,128)(2,1)} %bitcast.4, bf16[128,1152]{1,0:T(8,128)(2,1)} %bitcast.5, bf16[36,1152]{1,0:T(8,128)(2,1)} %wq_ref.1, bf16[36,1152]{1,0:T(8,128)(2,1)} %wk_ref.1, bf16[36,1152]{1,0:T(8,128)(2,1)} %wv_ref.1, bf16[36,1152]{1,0:T(8,128)(2,1)} %wo_ref.1), custom_call_target="tpu_custom_call" | custom-call | tf_op jit(solution)/shard_map/pallas_call | solution.py:615
  69.2 0.0 copy-start
  69.2 1.9 %convert_element_type.3 = f32[36,4608]{1,0:T(8,128)} convert(bf16[36,4608]{1,0:T(8,128)(2,1)} %get-tuple-element.5) | non-fusion elementwise | flops 165888 | bytes 995328 | tf_op jit(solution)/shard_map/convert_element_type | solution.py:638
  71.1 0.0 copy-done
  71.1 0.7 copy.9
Async XLA Ops:
  69.2 2.0 %copy-start = (bf16[128,1152]{1,0:T(8,128)(2,1)S(1)}, bf16[128,1152]{1,0:T(8,128)(2,1)}, u32[]{:S(2)}) copy-start(bf16[128,1152]{1,0:T(8,128)(2,1)} %get-tuple-element.4) | copy-start | bytes 884740

commit v5 on v4

--- a/solution.py
+++ b/solution.py
@@ -191,12 +191,13 @@
             k = 2 * ((zh + jnp.where(n < 2, n, 5 - n)) % ZH)
             p, q = col(k, xl), col(k + 1, xr)
             arrived(buf.at[p], rs, 8 + k)
-            around_x(buf, ss, rs, p, xr, 16).start()
+            around_x(buf, ss, rs, p, xr, 17).start()
             arrived(buf.at[q], rs, 9 + k)
-            around_x(buf, ss, rs, q, xl, 16).start()
+            around_x(buf, ss, rs, q, xl, 17).start()
 
     def rest(buf, rs):
-        arrived(buf.at[pl.ds(0, 16)], rs, 16)
+        arrived(buf.at[pl.ds(0, 8)], rs, 16)
+        arrived(buf.at[pl.ds(0, 8)], rs, 17)
 
     spread(WS, WL, 4, w_r)
     for s in sends[4:]:
@@ -204,9 +205,28 @@
     both_ways(WL, 4, w_r, 0, 2)
     hub_copy().wait_recv()
     spread(OH, OL, 6, o_r)
-    both_ways(WL, 4, w_r, 2, 4)
-    onward(WL, 4, w_r, 0, 2)
-    both_ways(WL, 4, w_r, 4, 8)
+    both_ways(WL, 4, w_r, 2, 6)
+    onward(WL, 4, w_r, 0, 1)
+    both_ways(WL, 4, w_r, 6, 8)
+
+    low16 = lanes(RP // 2) < 16
+
+    def unpack(xs):
+        for x2 in range(NX):
+            @pl.when(xs == x2)
+            def _():
+                @pl.loop(0, ZH)
+                def _(zs):
+                    out = WCAT.at[pl.ds(pl.multiple_of(zs * 288, 16), 288)]
+                    for cs in range(NC):
+                        p, base = (zs * NX + x2) * NC + cs, RP * (x2 * NC + cs)
+                        tl = WL[p, 3 * RP : 3 * RP + RP // 2, :].astype(F32)
+                        for s in range(3):
+                            out[base : base + RP, 256 * s : 256 * s + 128] = WL[p, RP * s : RP * s + RP, :]
+                            for half in range(2):
+                                v = jnp.where(low16, roll(tl, -(32 * s + 16 * half)), 0.0).astype(BF)
+                                at = base + half * (RP // 2)
+                                out[at : at + RP // 2, 256 * s + 128 : 256 * s + 256] = v
 
     def await_act(kind, yb):
         rcopy(blk(kind, yb, c), blk(kind, yb, c), sent.at[0], a_r.at[kind * 4 + yb], me).wait_recv()
@@ -227,25 +247,14 @@
     fwd[1].start()
     fwd[3].start()
     both_ways(OL, 6, o_r, 0, 8)
-    onward(WL, 4, w_r, 2, 4)
+    unpack(x)
+    onward(WL, 4, w_r, 1, 4)
     onward(OL, 6, o_r, 0, 4)
-    rest(WL, w_r)
-
-    low16 = lanes(RP // 2) < 16
-
-    @pl.loop(0, 8)
-    def _(g):
-        out = WCAT.at[pl.ds(pl.multiple_of(g * 144, 16), 144)]
-        for q in range(4):
-            p = g * 4 + q
-            base = RP * q
-            tl = WL[p, 3 * RP : 3 * RP + RP // 2, :].astype(F32)
-            for s in range(3):
-                out[base : base + RP, 256 * s : 256 * s + 128] = WL[p, RP * s : RP * s + RP, :]
-                for half in range(2):
-                    v = jnp.where(low16, roll(tl, -(32 * s + 16 * half)), 0.0).astype(BF)
-                    at = base + half * (RP // 2)
-                    out[at : at + RP // 2, 256 * s + 128 : 256 * s + 256] = v
+    arrived(WL.at[pl.ds(0, 8)], w_r, 16)
+    unpack(xl)
+    unpack(xr)
+    arrived(WL.at[pl.ds(0, 8)], w_r, 17)
+    unpack(xo)
 
     scale = 1.0 / HEAD_DIM**0.5
     row = lax.broadcasted_iota(jnp.int32, (ROWS, 128), 0)
@@ -285,9 +294,6 @@
             DQKV[i, rs, 256:512] = jnp.where(first, dk[:128], dk[128:]).astype(BF)
             dv = dot_nn(pb, g)
             DQKV[i, rs, 512:] = jnp.where(first, dv[:128], dv[128:]).astype(BF)
-        back = dot_nt(jnp.concatenate([DQKV[i] for i in ids], axis=0), WCAT[...]).astype(BF)
-        for m, i in enumerate(ids):
-            DXP[i] = back[256 * m : 256 * m + 256]
 
     await_act(1, left)
     fwd[4].start()
@@ -323,7 +329,7 @@
     def dx_sib(i):
         return rcopy(
             DXP.at[i, pl.ds(pl.multiple_of(sib * ROWS, ROWS), ROWS)], DXS.at[i],
-            sent.at[8], dx_r.at[0], (zh, x, sib, y, zl),
+            sent.at[8], dx_r.at[i], (zh, x, sib, y, zl),
         )
 
     @pl.loop(0, NY)
@@ -331,7 +337,7 @@
         off = jnp.where(n == 1, 3, jnp.where(n == 2, 1, jnp.where(n == 3, 2, 0)))
         i = (y + off) % NY
 
-        @pl.when(n == 2)
+        @pl.when(n == 1)
         def _():
             await_act(0, opp)
             fwd[6].start()
@@ -340,9 +346,8 @@
 
         await_sib(i)
         chunk((i,))
-        dx_sib(i).start()
-
-    OGRP, first_k = 4, (lambda h, side: 4 * side + h % 4)
+
+    OGRP, first_k = 4, (lambda h, side: 4 * side if h == 4 else (0, 1, 4, 5)[h] + 2 * side)
     bufs = lambda h: (DWO, OXA, OSM, ORL, ORR, O2S) if h == OGRP else (DWS, RXA, SMB, RL, RR, R2S)
 
     def some(h, side):
@@ -459,46 +464,53 @@
             (zh, x, c, (right, left)[side], zl),
         )
 
-    def dx_near(side):
-        return rcopy(
-            DXC.at[1 + side], DXR.at[side], sent.at[14], dx_r.at[1],
-            (zh, x, c, (right, left)[side], zl),
-        )
-
-    for i in (0, 1, 2, 4, 5, 6):
+    def dx_near(side, late):
+        at = 64 * side if late else 64 - 64 * side
+        i = (right, left)[side]
+        t = own_sum(i)[at : at + 64]
+        if late:
+            t = t + DXH[side].astype(F32)
+        DXC[1 + side, at : at + 64, :] = t.astype(BF)
+        rows = pl.ds(at, 64)
+        rcopy(
+            DXC.at[1 + side, rows], DXR.at[side, rows], sent.at[14], dx_r.at[4], (zh, x, c, i, zl)
+        ).start()
+
+    def dx_mat(i):
+        DXP[i] = dot_nt(DQKV[i], WCAT[...]).astype(BF)
+        dx_sib(i).start()
+
+    for i in range(5):
         dw_tile(i)
-    for g in (0, 1, 4, 5):
+    for g in range(4):
         pack(g)
     start_both(far, 0)
     start_both(near, 0)
     start_both(far, 1)
+    dx_mat(opp)
+    for i in range(5, 9):
+        dw_tile(i)
+    for g in range(4, 8):
+        pack(g)
+    start_both(far, 2)
     add_far(OGRP)
-    arrived(DXS, dx_r, 0)
+    dx_mat(right)
+    add_far(0)
+    start_both(near, 1)
+    dx_mat(left)
+    arrived(DXS.at[opp], dx_r, opp)
     DXC[0] = own_sum(opp).astype(BF)
     for side in range(2):
         dx_far(side).start()
-    for i in (3, 7, 8):
-        dw_tile(i)
-    for g in (2, 3, 6, 7):
-        pack(g)
-    start_both(far, 2)
-    add_far(0)
-    start_both(near, 1)
+    arrived(DXS.at[right], dx_r, right)
+    dx_near(0, False)
     add_far(1)
     start_both(far, 3)
     start_both(near, 2)
+    arrived(DXS.at[left], dx_r, left)
+    dx_near(1, False)
     send_z(OGRP)
-    for side in range(2):
-        dx_far(side).wait_recv()
-        t = own_sum((right, left)[side])
-        a, b = t[:64], t[64:]
-        if side == 0:
-            a = a + DXH[0].astype(F32)
-        else:
-            b = b + DXH[1].astype(F32)
-        DXC[1 + side, :64, :] = a.astype(BF)
-        DXC[1 + side, 64:, :] = b.astype(BF)
-        dx_near(side).start()
+    dx_mat(y)
     add_far(2)
     start_both(near, 3)
     send_z(0)
@@ -519,23 +531,27 @@
         b = FL.at[rep, part]
         return rcopy(b, b, sent.at[16 + o], f_r.at[o], (zh, x, c, r // ZL, r % ZL))
 
+    send_z(2)
+    send_z(3)
     FO[...] = z_sum(OGRP, OZ, O2S)
     home_copy().start()
-    send_z(2)
-    send_z(3)
+    for side in range(2):
+        dx_far(side).wait_recv()
+        dx_near(side, True)
+    FL[rep, :RA, :] = z_sum(0, RZ, R2S)
+
+    @pl.loop(1, NREP)
+    def _(dr):
+        fin(dr, head, 0).start()
+
     home_arrival().wait_recv()
 
     @pl.loop(1, NREP)
     def _(dr):
         fin(dr, foot, 1).start()
 
-    FL[rep, :RA, :] = z_sum(0, RZ, R2S)
-
-    @pl.loop(1, NREP)
-    def _(dr):
-        fin(dr, head, 0).start()
-
-    arrived(DXR, dx_r, 1)
+    arrived(DXS.at[y], dx_r, y)
+    arrived(DXR, dx_r, 4)
     GI[...] = (own_sum(y) + DXR[0].astype(F32) + DXR[1].astype(F32)).astype(BF)
     gi_out = pltpu.make_async_copy(GI, gi_ref, lsem.at[6])
     gi_out.start()
@@ -603,6 +619,20 @@
     gw_out.wait()
 
 
+def finish(gi_ref, gw_ref, gi_out, gw_out, GI, GW, GF, sem):
+    ins = [pltpu.make_async_copy(gw_ref, GW, sem.at[0]), pltpu.make_async_copy(gi_ref, GI, sem.at[1])]
+    outs = [pltpu.make_async_copy(GF, gw_out, sem.at[2]), pltpu.make_async_copy(GI, gi_out, sem.at[3])]
+    for i in ins:
+        i.start()
+    ins[0].wait()
+    GF[...] = GW[...].astype(F32)
+    outs[0].start()
+    ins[1].wait()
+    outs[1].start()
+    for o in outs:
+        o.wait()
+
+
 def vm(*shape, dtype=BF):
     return pltpu.VMEM(shape, dtype)
 
@@ -628,14 +658,25 @@
             vm(D, 768), vm(256, D), vm(NX, 8, RA, 128), *[vm(8, RA, 128)] * 5, vm(NZ, RA, 128),
             vm(NX, 8, RO, 128), *[vm(8, RO, 128)] * 5, vm(NZ, RO, 128),
             vm(RO, 128), vm(NREP, RF, 128), vm(ROWS, D), vm(RP, 4 * D),
-            dma(8), dma(20), dma(8), dma(4), dma(1), dma(17), dma(17), dma(2), dma(2), dma(10),
+            dma(8), dma(20), dma(8), dma(4), dma(1), dma(18), dma(18), dma(5), dma(2), dma(10),
             dma(5), dma(2), dma(1), dma(4),
         ],
         compiler_params=pltpu.CompilerParams(
             collective_id=0, has_side_effects=True, vmem_limit_bytes=60 * 2**20
         ),
     )(rows, drows, wq, wk, wv, wo)
-    return gi.reshape(tokens.shape), gw.astype(F32)
+    gi, gw = pl.pallas_call(
+        finish,
+        out_shape=(
+            jax.ShapeDtypeStruct((ROWS, D), BF),
+            jax.ShapeDtypeStruct((RP, 4 * D), F32),
+        ),
+        in_specs=[hbm] * 2,
+        out_specs=(hbm, hbm),
+        scratch_shapes=[vm(ROWS, D), vm(RP, 4 * D), vm(RP, 4 * D, dtype=F32), dma(4)],
+        compiler_params=pltpu.CompilerParams(vmem_limit_bytes=63 * 2**20),
+    )(gi, gw)
+    return gi.reshape(tokens.shape), gw
 
 
 def solution(mesh):

time: 72.9 us -> 67.9 us (0.931); the launches traced: 71.9 us -> 67.7 us
  other arithmetic: 1.94 us -> 0 us
  Pallas kernels: 68.6 us -> 67.1 us
    pallas_call x1, Pallas kernels: 68.6 us -> 65.1 us  [local(): pl.pallas_call(kernel, out_shape=(jax.ShapeDtypeStruct((ROWS, D), BF), ja...]
    pallas_call x0 -> x1, Pallas kernels: none -> 2.03 us  [local(): pl.pallas_call(finish, out_shape=(jax.ShapeDtypeStruct((ROWS, D), BF), ja...]
    convert_element_type x1 -> x0, other arithmetic: 1.94 us -> none  [local(): return (gi.reshape(tokens.shape), gw.astype(F32))]
where the time goes in v5:
time: 67.9 us; the launch traced here: 67.7 us
  Pallas kernels  67.1 us (99%)
    pallas_call x1, Pallas kernels, local(): pl.pallas_call(kernel, out_shape=(jax.ShapeDtypeStruct((ROWS, D), BF), ja...  65.1 us
    pallas_call x1, Pallas kernels, local(): pl.pallas_call(finish, out_shape=(jax.ShapeDtypeStruct((ROWS, D), BF), ja...  2.03 us

profile of v5, /device:TPU:1, one launch (start us, length us, event | category | flops | bytes accessed | tf_op | source)
XLA Modules:
  0.0 67.7 jit_solution(4791214278937397698)
XLA Ops:
  0.6 65.1 %shard_map.77 = (bf16[128,1152]{1,0:T(8,128)(2,1)}, bf16[36,4608]{1,0:T(8,128)(2,1)}) custom-call(bf16[128,1152]{1,0:T(8,128)(2,1)} %bitcast.3, bf16[128,1152]{1,0:T(8,128)(2,1)} %bitcast.4, bf16[36,1152]{1,0:T(8,128)(2,1)} %wq_ref.1, bf16[36,1152]{1,0:T(8,128)(2,1)} %wk_ref.1, bf16[36,1152]{1,0:T(8,128)(2,1)} %wv_ref.1, bf16[36,1152]{1,0:T(8,128)(2,1)} %wo_ref.1), custom_call_target="tpu_custom_call" | custom-call | tf_op jit(solution)/shard_map/pallas_call | solution.py:645
  65.7 2.0 %shard_map.78 = (bf16[128,1152]{1,0:T(8,128)(2,1)}, f32[36,4608]{1,0:T(8,128)}) custom-call(bf16[128,1152]{1,0:T(8,128)(2,1)} %get-tuple-element.6.gi_ref, bf16[36,4608]{1,0:T(8,128)(2,1)} %get-tuple-element.7.gw_ref), custom_call_target="tpu_custom_call" | custom-call | tf_op jit(solution)/shard_map/pallas_call | solution.py:668

commit v6 on v5

--- a/solution.py
+++ b/solution.py
@@ -102,24 +102,23 @@
     greet(hub)
     greet(home)
 
-    ii = lax.broadcasted_iota(jnp.int32, (D, 256), 0)
-    nn = lax.broadcasted_iota(jnp.int32, (D, 256), 1)
-    sel = jnp.where((ii == nn + COLS * rep) & (nn < COLS), 1.0, 0.0).astype(BF)
-    want = jnp.where(nn < 128, nn + 128 * rep, nn - 128 + 1024 + 16 * rep)
-    osel = jnp.where((ii == want) & (nn < COLS), 1.0, 0.0).astype(BF)
+    ii = lax.broadcasted_iota(jnp.int32, (256, 256), 0)
+    nn = lax.broadcasted_iota(jnp.int32, (256, 256), 1)
+    sel = jnp.where((ii == nn + 16 * rep) & (nn < COLS), 1.0, 0.0).astype(BF)
+    osel = jnp.where((ii == nn + 16 * rep) & (nn < 16), 1.0, 0.0).astype(BF)[:128, :128]
+    win = pl.multiple_of(128 * rep, 128)
     for w in wins:
         w.wait()
     tail = None
     for s in range(3):
-        b = dot_nn(WIN[s], sel)
+        b = dot_nn(WIN[s, :, pl.ds(win, 256)], sel)
         WS[RP * s : RP * s + RP, :] = b[:, :128].astype(BF)
         t = b[:, 128:256]
         t = roll(t[: RP // 2], 32 * s) + roll(t[RP // 2 :], 32 * s + 16)
         tail = t if tail is None else tail + t
     WS[3 * RP : 3 * RP + RP // 2, :] = tail.astype(BF)
-    b = dot_nn(WIN[3], osel)
-    OSRC[:RP, :] = b[:, :128].astype(BF)
-    t = b[:, 128:256]
+    OSRC[:RP, :] = WIN[3, :, pl.ds(win, 128)]
+    t = dot_nn(WIN[3, :, 1024:], osel)
     tail = t[:12] + roll(t[12:24], 16) + roll(t[24:36], 32)
     OSRC[RP : RP + 12, :] = tail.astype(BF)
     for o in own:
@@ -347,7 +346,7 @@
         await_sib(i)
         chunk((i,))
 
-    OGRP, first_k = 4, (lambda h, side: 4 * side if h == 4 else (0, 1, 4, 5)[h] + 2 * side)
+    OGRP, first_k = 4, (lambda h, side: 4 * side if h == 4 else 2 * h + side)
     bufs = lambda h: (DWO, OXA, OSM, ORL, ORR, O2S) if h == OGRP else (DWS, RXA, SMB, RL, RR, R2S)
 
     def some(h, side):
@@ -419,7 +418,8 @@
             t = t + buf[i].astype(F32)
         return t.astype(BF)
 
-    DWOB[...] = dot_tn(AS[...].reshape(NY * 256, 256), DA[...].reshape(NY * 256, D)).astype(BF)
+    attended = AS[...].reshape(NY * 256, 256)[:, :COLS]
+    DWOB[...] = dot_tn(attended, DA[...].reshape(NY * 256, D)).astype(BF)
     for q in range(4):
         tt = [DWOB[RP * q + 12 * t : RP * q + 12 * t + 12, 1024:1152].astype(F32) for t in range(3)]
         for r in range(NREP):
@@ -480,12 +480,16 @@
         DXP[i] = dot_nt(DQKV[i], WCAT[...]).astype(BF)
         dx_sib(i).start()
 
-    for i in range(5):
+    for i in range(3):
         dw_tile(i)
-    for g in range(4):
+    for g in range(2):
         pack(g)
     start_both(far, 0)
     start_both(near, 0)
+    for i in range(3, 5):
+        dw_tile(i)
+    for g in range(2, 4):
+        pack(g)
     start_both(far, 1)
     dx_mat(opp)
     for i in range(5, 9):
@@ -507,9 +511,9 @@
     add_far(1)
     start_both(far, 3)
     start_both(near, 2)
+    send_z(OGRP)
     arrived(DXS.at[left], dx_r, left)
     dx_near(1, False)
-    send_z(OGRP)
     dx_mat(y)
     add_far(2)
     start_both(near, 3)
@@ -531,13 +535,13 @@
         b = FL.at[rep, part]
         return rcopy(b, b, sent.at[16 + o], f_r.at[o], (zh, x, c, r // ZL, r % ZL))
 
+    for side in range(2):
+        dx_far(side).wait_recv()
+        dx_near(side, True)
     send_z(2)
     send_z(3)
     FO[...] = z_sum(OGRP, OZ, O2S)
     home_copy().start()
-    for side in range(2):
-        dx_far(side).wait_recv()
-        dx_near(side, True)
     FL[rep, :RA, :] = z_sum(0, RZ, R2S)
 
     @pl.loop(1, NREP)
@@ -655,7 +659,7 @@
             vm(RA, 128), vm(RO, 128), vm(RO, 128), vm(NPIX, RA, 128), vm(NPIX, RO, 128),
             vm(D, 768), vm(256, D), vm(NY, 256, 768), vm(NY, 256, 256),
             vm(NY, 256, D), vm(NY, ROWS, D), vm(3, ROWS, D), vm(2, 64, D), vm(2, ROWS, D),
-            vm(D, 768), vm(256, D), vm(NX, 8, RA, 128), *[vm(8, RA, 128)] * 5, vm(NZ, RA, 128),
+            vm(D, 768), vm(COLS, D), vm(NX, 8, RA, 128), *[vm(8, RA, 128)] * 5, vm(NZ, RA, 128),
             vm(NX, 8, RO, 128), *[vm(8, RO, 128)] * 5, vm(NZ, RO, 128),
             vm(RO, 128), vm(NREP, RF, 128), vm(ROWS, D), vm(RP, 4 * D),
             dma(8), dma(20), dma(8), dma(4), dma(1), dma(18), dma(18), dma(5), dma(2), dma(10),

time: 67.9 us -> 68.1 us (level)
  no operation moved by 1% of the time
where the time goes in v6:
time: 68.1 us; the launch traced here: 67.9 us
  Pallas kernels  67.3 us (99%)
    pallas_call x1, Pallas kernels, local(): pl.pallas_call(kernel, out_shape=(jax.ShapeDtypeStruct((ROWS, D), BF), ja...  65.3 us
    pallas_call x1, Pallas kernels, local(): pl.pallas_call(finish, out_shape=(jax.ShapeDtypeStruct((ROWS, D), BF), ja...  2.03 us

profile of v6, /device:TPU:1, one launch (start us, length us, event | category | flops | bytes accessed | tf_op | source)
XLA Modules:
  0.0 67.9 jit_solution(9489813028569492479)
XLA Ops:
  0.6 65.3 %shard_map.77 = (bf16[128,1152]{1,0:T(8,128)(2,1)}, bf16[36,4608]{1,0:T(8,128)(2,1)}) custom-call(bf16[128,1152]{1,0:T(8,128)(2,1)} %bitcast.3, bf16[128,1152]{1,0:T(8,128)(2,1)} %bitcast.4, bf16[36,1152]{1,0:T(8,128)(2,1)} %wq_ref.1, bf16[36,1152]{1,0:T(8,128)(2,1)} %wk_ref.1, bf16[36,1152]{1,0:T(8,128)(2,1)} %wv_ref.1, bf16[36,1152]{1,0:T(8,128)(2,1)} %wo_ref.1), custom_call_target="tpu_custom_call" | custom-call | tf_op jit(solution)/shard_map/pallas_call | solution.py:649
  65.9 2.0 %shard_map.78 = (bf16[128,1152]{1,0:T(8,128)(2,1)}, f32[36,4608]{1,0:T(8,128)}) custom-call(bf16[128,1152]{1,0:T(8,128)(2,1)} %get-tuple-element.6.gi_ref, bf16[36,4608]{1,0:T(8,128)(2,1)} %get-tuple-element.7.gw_ref), custom_call_target="tpu_custom_call" | custom-call | tf_op jit(solution)/shard_map/pallas_call | solution.py:672

commit v7 on v6

--- a/solution.py
+++ b/solution.py
@@ -346,7 +346,7 @@
         await_sib(i)
         chunk((i,))
 
-    OGRP, first_k = 4, (lambda h, side: 4 * side if h == 4 else 2 * h + side)
+    OGRP, first_k = 4, (lambda h, side: 4 * side if h == 4 else (0, 1, 4, 5)[h] + 2 * side)
     bufs = lambda h: (DWO, OXA, OSM, ORL, ORR, O2S) if h == OGRP else (DWS, RXA, SMB, RL, RR, R2S)
 
     def some(h, side):
@@ -480,16 +480,12 @@
         DXP[i] = dot_nt(DQKV[i], WCAT[...]).astype(BF)
         dx_sib(i).start()
 
-    for i in range(3):
+    for i in range(5):
         dw_tile(i)
-    for g in range(2):
+    for g in range(4):
         pack(g)
     start_both(far, 0)
     start_both(near, 0)
-    for i in range(3, 5):
-        dw_tile(i)
-    for g in range(2, 4):
-        pack(g)
     start_both(far, 1)
     dx_mat(opp)
     for i in range(5, 9):
@@ -511,9 +507,9 @@
     add_far(1)
     start_both(far, 3)
     start_both(near, 2)
-    send_z(OGRP)
     arrived(DXS.at[left], dx_r, left)
     dx_near(1, False)
+    send_z(OGRP)
     dx_mat(y)
     add_far(2)
     start_both(near, 3)
@@ -535,13 +531,13 @@
         b = FL.at[rep, part]
         return rcopy(b, b, sent.at[16 + o], f_r.at[o], (zh, x, c, r // ZL, r % ZL))
 
-    for side in range(2):
-        dx_far(side).wait_recv()
-        dx_near(side, True)
     send_z(2)
     send_z(3)
     FO[...] = z_sum(OGRP, OZ, O2S)
     home_copy().start()
+    for side in range(2):
+        dx_far(side).wait_recv()
+        dx_near(side, True)
     FL[rep, :RA, :] = z_sum(0, RZ, R2S)
 
     @pl.loop(1, NREP)

time: 68.1 us -> 67.5 us (level)
  no operation moved by 1% of the time
where the time goes in v7:
time: 67.5 us; the launch traced here: 67.4 us
  Pallas kernels  66.7 us (99%)
    pallas_call x1, Pallas kernels, local(): pl.pallas_call(kernel, out_shape=(jax.ShapeDtypeStruct((ROWS, D), BF), ja...  64.7 us
    pallas_call x1, Pallas kernels, local(): pl.pallas_call(finish, out_shape=(jax.ShapeDtypeStruct((ROWS, D), BF), ja...  2.03 us

profile of v7, /device:TPU:1, one launch (start us, length us, event | category | flops | bytes accessed | tf_op | source)
XLA Modules:
  0.0 67.4 jit_solution(2823935015305885980)
XLA Ops:
  0.6 64.7 %shard_map.77 = (bf16[128,1152]{1,0:T(8,128)(2,1)}, bf16[36,4608]{1,0:T(8,128)(2,1)}) custom-call(bf16[128,1152]{1,0:T(8,128)(2,1)} %bitcast.3, bf16[128,1152]{1,0:T(8,128)(2,1)} %bitcast.4, bf16[36,1152]{1,0:T(8,128)(2,1)} %wq_ref.1, bf16[36,1152]{1,0:T(8,128)(2,1)} %wk_ref.1, bf16[36,1152]{1,0:T(8,128)(2,1)} %wv_ref.1, bf16[36,1152]{1,0:T(8,128)(2,1)} %wo_ref.1), custom_call_target="tpu_custom_call" | custom-call | tf_op jit(solution)/shard_map/pallas_call | solution.py:645
  65.4 2.0 %shard_map.78 = (bf16[128,1152]{1,0:T(8,128)(2,1)}, f32[36,4608]{1,0:T(8,128)}) custom-call(bf16[128,1152]{1,0:T(8,128)(2,1)} %get-tuple-element.6.gi_ref, bf16[36,4608]{1,0:T(8,128)(2,1)} %get-tuple-element.7.gw_ref), custom_call_target="tpu_custom_call" | custom-call | tf_op jit(solution)/shard_map/pallas_call | solution.py:668

commit v8 on v6

--- a/solution.py
+++ b/solution.py
@@ -511,9 +511,9 @@
     add_far(1)
     start_both(far, 3)
     start_both(near, 2)
-    send_z(OGRP)
     arrived(DXS.at[left], dx_r, left)
     dx_near(1, False)
+    send_z(OGRP)
     dx_mat(y)
     add_far(2)
     start_both(near, 3)
@@ -535,13 +535,13 @@
         b = FL.at[rep, part]
         return rcopy(b, b, sent.at[16 + o], f_r.at[o], (zh, x, c, r // ZL, r % ZL))
 
-    for side in range(2):
-        dx_far(side).wait_recv()
-        dx_near(side, True)
     send_z(2)
     send_z(3)
     FO[...] = z_sum(OGRP, OZ, O2S)
     home_copy().start()
+    for side in range(2):
+        dx_far(side).wait_recv()
+        dx_near(side, True)
     FL[rep, :RA, :] = z_sum(0, RZ, R2S)
 
     @pl.loop(1, NREP)
@@ -557,7 +557,7 @@
     arrived(DXS.at[y], dx_r, y)
     arrived(DXR, dx_r, 4)
     GI[...] = (own_sum(y) + DXR[0].astype(F32) + DXR[1].astype(F32)).astype(BF)
-    gi_out = pltpu.make_async_copy(GI, gi_ref, lsem.at[6])
+    gi_out = pltpu.make_async_copy(GI, gi_ref, lsem.at[0])
     gi_out.start()
 
     def left_from(ref, idx):
@@ -617,7 +617,7 @@
             v = roll(jnp.where(lane12 // 16 == t, tl, 0.0), 16 * (r - t))
             parts[t] = v if parts[t] is None else parts[t] + v
     GW[:, 3 * D + 1024 :] = jnp.concatenate(parts, axis=0).astype(GW.dtype)
-    gw_out = pltpu.make_async_copy(GW, gw_ref, lsem.at[7])
+    gw_out = pltpu.make_async_copy(GW, gw_ref, lsem.at[1])
     gw_out.start()
     gi_out.wait()
     gw_out.wait()
@@ -662,8 +662,8 @@
             vm(D, 768), vm(COLS, D), vm(NX, 8, RA, 128), *[vm(8, RA, 128)] * 5, vm(NZ, RA, 128),
             vm(NX, 8, RO, 128), *[vm(8, RO, 128)] * 5, vm(NZ, RO, 128),
             vm(RO, 128), vm(NREP, RF, 128), vm(ROWS, D), vm(RP, 4 * D),
-            dma(8), dma(20), dma(8), dma(4), dma(1), dma(18), dma(18), dma(5), dma(2), dma(10),
-            dma(5), dma(2), dma(1), dma(4),
+            dma(6), dma(18), dma(8), dma(4), dma(1), dma(18), dma(18), dma(5), dma(2), dma(10),
+            dma(5), dma(2), dma(1), dma(2),
         ],
         compiler_params=pltpu.CompilerParams(
             collective_id=0, has_side_effects=True, vmem_limit_bytes=60 * 2**20

time: 68.1 us -> 67.7 us (level)
  no operation moved by 1% of the time
where the time goes in v8:
time: 67.7 us; the launch traced here: 67.6 us
  Pallas kernels  66.9 us (99%)
    pallas_call x1, Pallas kernels, local(): pl.pallas_call(kernel, out_shape=(jax.ShapeDtypeStruct((ROWS, D), BF), ja...  64.9 us
    pallas_call x1, Pallas kernels, local(): pl.pallas_call(finish, out_shape=(jax.ShapeDtypeStruct((ROWS, D), BF), ja...  2.03 us

profile of v8, /device:TPU:1, one launch (start us, length us, event | category | flops | bytes accessed | tf_op | source)
XLA Modules:
  0.0 67.6 jit_solution(15245278221676725308)
XLA Ops:
  0.6 64.9 %shard_map.77 = (bf16[128,1152]{1,0:T(8,128)(2,1)}, bf16[36,4608]{1,0:T(8,128)(2,1)}) custom-call(bf16[128,1152]{1,0:T(8,128)(2,1)} %bitcast.3, bf16[128,1152]{1,0:T(8,128)(2,1)} %bitcast.4, bf16[36,1152]{1,0:T(8,128)(2,1)} %wq_ref.1, bf16[36,1152]{1,0:T(8,128)(2,1)} %wk_ref.1, bf16[36,1152]{1,0:T(8,128)(2,1)} %wv_ref.1, bf16[36,1152]{1,0:T(8,128)(2,1)} %wo_ref.1), custom_call_target="tpu_custom_call" | custom-call | tf_op jit(solution)/shard_map/pallas_call | solution.py:649
  65.6 2.0 %shard_map.78 = (bf16[128,1152]{1,0:T(8,128)(2,1)}, f32[36,4608]{1,0:T(8,128)}) custom-call(bf16[128,1152]{1,0:T(8,128)(2,1)} %get-tuple-element.6.gi_ref, bf16[36,4608]{1,0:T(8,128)(2,1)} %get-tuple-element.7.gw_ref), custom_call_target="tpu_custom_call" | custom-call | tf_op jit(solution)/shard_map/pallas_call | solution.py:672
